TPU v7x, 32 devices: a whole 2x2x4 slice. The times are simulated.
32 devices in a mesh: shard: 8 (over y, x, core), dp: 4 (over z).
Axes of the slice: x: 2, y: 2, z: 4, core: 2. Of those that a mesh axis runs over, the one named last changes fastest.
Arguments:
- grad: float32 [288, 128, 4096], P('shard', 'dp'), may hold values from -252 to 252
- param: bfloat16 [288, 128, 4096], P('shard', 'dp'), may hold values from -0.119628906 to 0.119628906
- row_state: float32 [288, 128], P('shard', 'dp'), may hold values from 0.3 to 27
- col_state: float32 [3, 4096], replicated, may hold values from 0.002 to 400
- block_start: int32 [8], replicated, may hold values from 0 to 143, as said below
- block_matrix: int32 [144], replicated, may hold values from 0 to 2, as said below
- step: int32 [1], replicated, may hold values from 2 to 11
Outputs:
- new_params: bfloat16 [18432, 4096], P(None, 'shard')
- new_row_state: float32 [288, 128], P('shard', 'dp')
- new_col_state: float32 [3, 4096], replicated
Inputs may be any that keep to these rules, and one draw needn't show every extreme that they name: block_start rises from 0 at index 0; every shard index owns between 1 and 36 consecutive global blocks, held in its first slots, and some index owns exactly 36; slots past a device's owned count hold values that no output reads. `block_matrix`: ids 0 and 1 each label 4096 / 128 blocks and id 2 labels 10240 / 128 blocks, in any order.
All inputs are finite; a program needn't handle non-finite values.
Results may differ from a plain program's by a relative error of at most 0.0004.
Values may be sent and summed in bfloat16 or wider, within the bound.
A program may use at most 192 MiB of HBM per device.

v0:
```python
import functools

import jax
import jax.numpy as jnp
from jax import lax
from jax.experimental import pallas as pl
from jax.experimental.pallas import tpu as pltpu
from jax.sharding import PartitionSpec as P

D = 4096
FF = 10240
MATS = 3
CHUNK = 8


def slots_per_step(slot_count):
    return max(n for n in range(1, 5) if slot_count % n == 0)


def sums_kernel(group, mats, piece, ints_ref, floats_ref, grad_ref, state_ref, rows_ref, sums_ref, cols_acc, weighted_acc, rows_acc):
    step = pl.program_id(0)
    owned = ints_ref[0]
    beta = floats_ref[0]
    gain = floats_ref[1]
    height, width = grad_ref.shape[1], grad_ref.shape[2]

    @pl.when(step == 0)
    def _():
        cols_acc[...] = jnp.zeros_like(cols_acc)
        weighted_acc[...] = jnp.zeros_like(weighted_acc)
        rows_acc[...] = jnp.zeros_like(rows_acc)

    for j in range(group):
        slot = step * group + j

        @pl.when(slot >= owned)
        def _():
            rows_ref[j] = jnp.zeros_like(rows_ref[j])

        @pl.when(slot < owned)
        def _():
            m = ints_ref[2 + slot]
            squares = grad_ref[j] * grad_ref[j]
            rows = beta * state_ref[j] + gain * jnp.sum(squares, axis=1, keepdims=True)
            rows_ref[j] = rows
            tall = (height // 8, 8, width)
            cols_acc[m] += jnp.sum(squares.reshape(tall), axis=0)
            weighted_acc[m] += jnp.sum((squares * (1.0 / rows)).reshape(tall), axis=0)
            rows_acc[m] += jnp.sum(jnp.broadcast_to(rows, (height, 128)).reshape(height // 8, 8, 128), axis=0)

    @pl.when(step == pl.num_programs(0) - 1)
    def _():
        sums_ref[...] = jnp.zeros_like(sums_ref)
        for m in range(mats):
            sums_ref[m : m + 1, :] = jnp.sum(cols_acc[m], axis=0, keepdims=True)
            sums_ref[mats + m : mats + m + 1, :] = jnp.sum(weighted_acc[m], axis=0, keepdims=True)
            spot = lax.broadcasted_iota(jnp.int32, (1, sums_ref.shape[1]), 1) % piece == m
            part = jnp.sum(rows_acc[m], axis=0, keepdims=True)[:, 0:1]
            sums_ref[2 * mats : 2 * mats + 1, :] += jnp.where(spot, part, 0.0)


def update_kernel(group, mats, parts, row_counts, ints_ref, floats_ref, grad_ref, param_ref, rows_ref, total_ref, state_ref, *refs):
    chunk_refs, (cols_ref, factor) = refs[:-2], refs[-2:]
    step = pl.program_id(0)
    owned, last = ints_ref[0], ints_ref[1]
    beta, rest, rate = floats_ref[0], floats_ref[2], floats_ref[3]
    height, width = grad_ref.shape[1], grad_ref.shape[2]
    cut = width // parts

    @pl.when(step == 0)
    def _():
        for m in range(mats):
            count = row_counts[m]
            cols = beta * state_ref[m : m + 1, :] + rest * (total_ref[m : m + 1, :] / count)
            cols_ref[m : m + 1, :] = cols
            average = total_ref[2 * mats : 2 * mats + 1, m : m + 1] / count
            weighted = total_ref[mats + m : mats + m + 1, :]
            square = average * jnp.sum(weighted / cols, axis=1, keepdims=True)
            clip = jnp.maximum(1.0, jnp.sqrt(square / (count * width)))
            factor[m] = lax.rsqrt(cols) * (jnp.sqrt(average) * rate / clip)

    @pl.when(step <= last)
    def _():
        for j in range(group):
            slot = step * group + j

            @pl.when(slot < owned)
            def _():
                m = ints_ref[2 + slot]
                scale = lax.rsqrt(rows_ref[j])
                for k, chunk_ref in enumerate(chunk_refs):
                    at = slice(k * CHUNK, (k + 1) * CHUNK)
                    for n in range(parts):
                        span = slice(n * cut, (n + 1) * cut)
                        new = param_ref[j, at, span].astype(jnp.float32) - grad_ref[j, at, span] * scale[at] * factor[m, :, span]
                        chunk_ref[n, j] = new.astype(chunk_ref.dtype)


def pick_kernel(slot_ref, in_ref, out_ref):
    def move(b, carry):
        out_ref[b] = in_ref[slot_ref[b]]
        return carry

    lax.fori_loop(0, out_ref.shape[0], move, 0, unroll=8)


def place_kernel(in_ref, *refs):
    refs[-1][:, :, 0] = in_ref[...]


def body(parts, grad, param, row_state, col_state, block_start, block_matrix, step):
    slot_count, height, width = grad.shape
    mats = col_state.shape[0]
    total_blocks = block_matrix.shape[0]
    group = slots_per_step(slot_count)
    steps = slot_count // group
    chunks = height // CHUNK
    cut = width // parts
    every = lax.axis_size(("shard", "dp"))
    piece = width // every
    row_counts = (float(D), float(D), float(FF))

    shard_index = lax.axis_index("shard")
    block_ends = jnp.concatenate([block_start[1:], jnp.full((1,), total_blocks, jnp.int32)])
    at_shard = jnp.arange(parts, dtype=jnp.int32) == shard_index
    first_block = jnp.sum(jnp.where(at_shard, block_start, 0))
    owned = jnp.sum(jnp.where(at_shard, block_ends - block_start, 0))
    block_index = jnp.arange(total_blocks, dtype=jnp.int32)
    slot_blocks = first_block + jnp.arange(slot_count, dtype=jnp.int32)
    matrix_ids = jnp.sum(
        jnp.where(slot_blocks[:, None] == block_index[None, :], block_matrix[None, :], 0), axis=1
    )
    started = block_start[None, :] <= block_index[:, None]
    owner = jnp.sum(started.astype(jnp.int32), axis=1) - 1
    owner_start = jnp.max(jnp.where(started, block_start[None, :], 0), axis=1)
    slot_of = owner * slot_count + block_index - owner_start
    ints = jnp.concatenate([jnp.stack([owned, (owned - 1) // group]), matrix_ids]).astype(jnp.int32)
    step_value = step[0].astype(jnp.float32)
    beta = 1.0 - step_value ** (-0.8)
    rate = 1.0 / jnp.sqrt(jnp.maximum(step_value, 10000.0))
    floats = jnp.stack([beta, (1.0 - beta) / width, 1.0 - beta, rate])

    smem = pl.BlockSpec(memory_space=pltpu.SMEM)

    def live(i, ints_ref):
        return jnp.minimum(i, ints_ref[1])

    new_rows, sums = pl.pallas_call(
        functools.partial(sums_kernel, group, mats, piece),
        grid_spec=pltpu.PrefetchScalarGridSpec(
            num_scalar_prefetch=1,
            grid=(steps,),
            in_specs=[
                smem,
                pl.BlockSpec((group, height, width), lambda i, s: (live(i, s), 0, 0)),
                pl.BlockSpec((group, height, 1), lambda i, s: (i, 0, 0)),
            ],
            out_specs=[
                pl.BlockSpec((group, height, 1), lambda i, s: (i, 0, 0)),
                pl.BlockSpec((8, width), lambda i, s: (0, 0)),
            ],
            scratch_shapes=[
                pltpu.VMEM((mats, 8, width), jnp.float32),
                pltpu.VMEM((mats, 8, width), jnp.float32),
                pltpu.VMEM((mats, 8, 128), jnp.float32),
            ],
        ),
        out_shape=[
            jax.ShapeDtypeStruct((slot_count, height, 1), jnp.float32),
            jax.ShapeDtypeStruct((8, width), jnp.float32),
        ],
        compiler_params=pltpu.CompilerParams(vmem_limit_bytes=60 * 2**20),
        cost_estimate=pl.CostEstimate(flops=grad.size * 6, bytes_accessed=grad.size * 4, transcendentals=0),
        name="sums",
    )(ints, floats, grad, row_state[:, :, None])

    pieces = sums.reshape(8, every, piece).transpose(1, 0, 2)
    pieces = lax.all_to_all(pieces, ("shard", "dp"), split_axis=0, concat_axis=0, tiled=True)
    total = lax.all_gather(jnp.sum(pieces, axis=0), ("shard", "dp"), axis=0)
    total = total.transpose(1, 0, 2).reshape(8, width)

    outs = pl.pallas_call(
        functools.partial(update_kernel, group, mats, parts, row_counts),
        grid_spec=pltpu.PrefetchScalarGridSpec(
            num_scalar_prefetch=1,
            grid=(steps,),
            in_specs=[
                smem,
                pl.BlockSpec((group, height, width), lambda i, s: (live(i, s), 0, 0)),
                pl.BlockSpec((group, height, width), lambda i, s: (live(i, s), 0, 0)),
                pl.BlockSpec((group, height, 1), lambda i, s: (live(i, s), 0, 0)),
                pl.BlockSpec((8, width), lambda i, s: (0, 0)),
                pl.BlockSpec((mats, width), lambda i, s: (0, 0)),
            ],
            out_specs=[
                pl.BlockSpec((parts, group, CHUNK, cut), lambda i, s: (0, live(i, s), 0, 0))
                for _ in range(chunks)
            ]
            + [pl.BlockSpec((mats, width), lambda i, s: (0, 0))],
            scratch_shapes=[pltpu.VMEM((mats, 1, width), jnp.float32)],
        ),
        out_shape=[
            jax.ShapeDtypeStruct((parts, slot_count, CHUNK, cut), jnp.bfloat16) for _ in range(chunks)
        ]
        + [jax.ShapeDtypeStruct((mats, width), jnp.float32)],
        compiler_params=pltpu.CompilerParams(vmem_limit_bytes=60 * 2**20),
        cost_estimate=pl.CostEstimate(flops=grad.size * 6, bytes_accessed=grad.size * 8, transcendentals=0),
        name="update",
    )(ints, floats, grad, param, new_rows, total, col_state)
    new_cols = outs[-1]

    dp = lax.axis_size("dp")
    piece_bytes = total_blocks * CHUNK * cut * 2
    placed = None
    run = 12 if total_blocks % 12 == 0 else 1
    for k in range(chunks):
        moved = lax.all_to_all(outs[k], "shard", split_axis=0, concat_axis=0, tiled=True)
        picked = pl.pallas_call(
            pick_kernel,
            in_specs=[smem, pl.BlockSpec(memory_space=pltpu.VMEM)],
            out_specs=pl.BlockSpec(memory_space=pltpu.VMEM),
            out_shape=jax.ShapeDtypeStruct((total_blocks, CHUNK, cut), jnp.bfloat16),
            compiler_params=pltpu.CompilerParams(vmem_limit_bytes=16 * 2**20),
            cost_estimate=pl.CostEstimate(flops=0, bytes_accessed=3 * piece_bytes, transcendentals=0),
            name="pick",
        )(slot_of, moved.reshape(parts * slot_count, CHUNK, cut))
        spread = lax.all_gather(picked, "dp", axis=1, tiled=True)
        spread = spread.reshape(total_blocks, dp, CHUNK, cut)
        old = [] if placed is None else [placed]
        placed = pl.pallas_call(
            place_kernel,
            grid=(total_blocks // run,),
            in_specs=[pl.BlockSpec((run, dp, CHUNK, cut), lambda i: (i, 0, 0, 0))]
            + [pl.BlockSpec(memory_space=pl.ANY) for _ in old],
            out_specs=pl.BlockSpec((run, dp, 1, CHUNK, cut), functools.partial(lambda k, i: (i, 0, k, 0, 0), k)),
            out_shape=jax.ShapeDtypeStruct((total_blocks, dp, chunks, CHUNK, cut), jnp.bfloat16),
            input_output_aliases={1: 0} if old else {},
            compiler_params=pltpu.CompilerParams(vmem_limit_bytes=60 * 2**20),
            cost_estimate=pl.CostEstimate(flops=0, bytes_accessed=2 * dp * piece_bytes, transcendentals=0),
            name="place",
        )(spread, *old)
    new_params = placed.reshape(total_blocks * dp * height, cut)
    return new_params, new_rows[:, :, 0], new_cols


def solution(mesh):
    return jax.shard_map(
        functools.partial(body, mesh.shape["shard"]),
        mesh=mesh,
        in_specs=(
            P("shard", "dp", None),
            P("shard", "dp", None),
            P("shard", "dp"),
            P(),
            P(),
            P(),
            P(),
        ),
        out_specs=(P(None, "shard"), P("shard", "dp"), P()),
        check_vma=False,
    )
```

profile of v0, /device:TPU:0, one launch (start us, length us, event | category | flops | bytes accessed | tf_op | source)
XLA Modules:
  0.0 537.6 jit_solution(6129296501298714419)
XLA Ops:
  7.2 0.7 slice.3
  7.9 1.4 fusion
  9.9 0.7 iota_add_fusion
  11.3 2.1 copy.17.state_ref
  13.4 0.9 select_reduce_fusion
  14.3 0.6 pad_maximum_fusion.floats_ref
  14.9 1.3 pad_add_fusion.ints_ref
  16.2 13.6 %sums.1 = (f32[36,32,1]{2,1,0:T(8,128)}, f32[8,4096]{1,0:T(8,128)}) custom-call(s32[38]{0:T(128)} %pad_add_fusion.ints_ref, f32[4]{0:T(128)} %pad_maximum_fusion.floats_ref, f32[36,32,4096]{2,1,0:T(8,128)} %grad_ref.3, f32[36,32,1]{2,1,0:T(8,128)} %copy.17.state_ref), custom_call_target="tpu_custom_call" | custom-call | flops 28311552 | bytes 18874368 | tf_op jit(solution)/shard_map/sums/pallas_call | solution.py:148
  29.8 16.4 %all_to_all.25 = f32[32,8,128]{2,1,0:T(8,128)S(1)} all-to-all(f32[32,8,128]{2,1,0:T(8,128)} %bitcast.31), channel_id=1, replica_groups=mesh['shard'=8,'dp'=4] {'shard','dp'}, dimensions={0} | all-to-all | bytes 262144 | tf_op jit(solution)/shard_map/all_to_all | solution.py:178
  46.2 69.9 %all-gather = f32[256,128]{1,0:T(8,128)} all-gather(f32[8,128]{1,0:T(8,128)S(1)} %reduce_sum.49), channel_id=2, replica_groups=mesh['shard'=8,'dp'=4] {'shard','dp'}, dimensions={0}, use_global_device_ids=true | all-gather | bytes 135168 | tf_op jit(solution)/shard_map/all_gather | solution.py:179
  116.2 15.8 %update.1 = (bf16[8,36,8,512]{3,2,1,0:T(8,128)(2,1)}, bf16[8,36,8,512]{3,2,1,0:T(8,128)(2,1)}, bf16[8,36,8,512]{3,2,1,0:T(8,128)(2,1)}, bf16[8,36,8,512]{3,2,1,0:T(8,128)(2,1)}, f32[3,4096]{1,0:T(4,128)}) custom-call(s32[38]{0:T(128)} %pad_add_fusion.ints_ref, f32[4]{0:T(128)} %pad_maximum_fusion.floats_ref, f32[36,32,4096]{2,1,0:T(8,128)} %grad_ref.3, ...), custom_call_target="tpu_custom_call" | custom-call | flops 28311552 | bytes 37748736 | tf_op jit(solution)/shard_map/update/pallas_call | solution.py:182
  132.0 5.0 all-to-all-start.4
  137.1 0.1 convert_reduce_fusion
  137.2 29.3 %all-to-all-done.4 = bf16[8,36,8,512]{3,2,1,0:T(8,128)(2,1)S(1)} async-done(((bf16[8,36,8,512]{3,2,1,0:T(8,128)(2,1)}), bf16[8,36,8,512]{3,2,1,0:T(8,128)(2,1)S(1)}, u32[]{:S(2)}, u32[]{:S(2)}) %all-to-all-start.4) | async-done | bytes 2359328 | tf_op jit(solution)/shard_map/all_to_all | solution.py:217
  166.4 1.8 pick.7
  168.3 0.0 all-gather.10.cloned.1.call-start
  168.3 32.9 %all_to_all.26 = bf16[8,36,8,512]{3,2,1,0:T(8,128)(2,1)S(1)} all-to-all(bf16[8,36,8,512]{3,2,1,0:T(8,128)(2,1)} %get-tuple-element.14), channel_id=1, replica_groups=mesh['shard'=8,'dp'=4] {'shard'}, dimensions={0} | all-to-all | bytes 4718592 | tf_op jit(solution)/shard_map/all_to_all | solution.py:217
  201.2 1.8 pick.6
  203.1 0.0 all-gather.8.cloned.1.call-start
  203.1 31.8 %all_to_all.27 = bf16[8,36,8,512]{3,2,1,0:T(8,128)(2,1)S(1)} all-to-all(bf16[8,36,8,512]{3,2,1,0:T(8,128)(2,1)S(1)} %copy-done.1), channel_id=1, replica_groups=mesh['shard'=8,'dp'=4] {'shard'}, dimensions={0} | all-to-all | bytes 4718592 | tf_op jit(solution)/shard_map/all_to_all | solution.py:217
  235.0 1.8 pick.5
  236.8 0.0 all-gather.6.cloned.1.call-start
  236.9 31.8 %all_to_all.28 = bf16[8,36,8,512]{3,2,1,0:T(8,128)(2,1)S(1)} all-to-all(bf16[8,36,8,512]{3,2,1,0:T(8,128)(2,1)S(1)} %copy-done), channel_id=1, replica_groups=mesh['shard'=8,'dp'=4] {'shard'}, dimensions={0} | all-to-all | bytes 4718592 | tf_op jit(solution)/shard_map/all_to_all | solution.py:217
  268.7 1.9 pick.4
  270.6 1.0 copy.18
  271.6 8.5 %place.4.refs_0_ = bf16[144,4,4,8,512]{4,3,2,1,0:T(8,128)(2,1)} custom-call(bf16[144,4,8,512]{3,2,1,0:T(8,128)(2,1)} %bitcast.26), custom_call_target="tpu_custom_call" | custom-call | bytes 9437184 | tf_op jit(solution)/shard_map/place/pallas_call | solution.py:230
  280.1 63.8 %all-gather.10.cloned.1.call-done = bf16[144,32,512]{2,1,0:T(8,128)(2,1)} async-done(((bf16[144,8,512]{2,1,0:T(8,128)(2,1)}), bf16[144,32,512]{2,1,0:T(8,128)(2,1)}) %all-gather.10.cloned.1.call-update) | async-done | bytes 4718608 | tf_op jit(solution)/shard_map/all_gather | solution.py:227
  343.9 8.6 %place.5.refs_0_ = bf16[144,4,4,8,512]{4,3,2,1,0:T(8,128)(2,1)} custom-call(bf16[144,4,8,512]{3,2,1,0:T(8,128)(2,1)} %bitcast.27, bf16[144,4,4,8,512]{4,3,2,1,0:T(8,128)(2,1)} %place.4.refs_0_), custom_call_target="tpu_custom_call", output_to_operand_aliasing={{}: (1, {})} | custom-call | bytes 9437184 | tf_op jit(solution)/shard_map/place/pallas_call | solution.py:230
  352.6 80.8 %all-gather.8.cloned.1.call-done = bf16[144,32,512]{2,1,0:T(8,128)(2,1)} async-done(((bf16[144,8,512]{2,1,0:T(8,128)(2,1)}), bf16[144,32,512]{2,1,0:T(8,128)(2,1)}) %all-gather.8.cloned.1.call-update) | async-done | bytes 4718608 | tf_op jit(solution)/shard_map/all_gather | solution.py:227
  433.4 8.6 %place.6.refs_0_ = bf16[144,4,4,8,512]{4,3,2,1,0:T(8,128)(2,1)} custom-call(bf16[144,4,8,512]{3,2,1,0:T(8,128)(2,1)} %bitcast.28, bf16[144,4,4,8,512]{4,3,2,1,0:T(8,128)(2,1)} %place.5.refs_0_), custom_call_target="tpu_custom_call", output_to_operand_aliasing={{}: (1, {})} | custom-call | bytes 9437184 | tf_op jit(solution)/shard_map/place/pallas_call | solution.py:230
  442.0 80.6 %all-gather.6.cloned.1.call-done = bf16[144,32,512]{2,1,0:T(8,128)(2,1)} async-done(((bf16[144,8,512]{2,1,0:T(8,128)(2,1)}), bf16[144,32,512]{2,1,0:T(8,128)(2,1)}) %all-gather.6.cloned.1.call-update) | async-done | bytes 4718608 | tf_op jit(solution)/shard_map/all_gather | solution.py:227
  522.6 8.5 %place.7 = bf16[144,4,4,8,512]{4,3,2,1,0:T(8,128)(2,1)} custom-call(bf16[144,4,8,512]{3,2,1,0:T(8,128)(2,1)} %bitcast.29, bf16[144,4,4,8,512]{4,3,2,1,0:T(8,128)(2,1)} %place.6.refs_0_), custom_call_target="tpu_custom_call", output_to_operand_aliasing={{}: (1, {})} | custom-call | bytes 9437184 | tf_op jit(solution)/shard_map/place/pallas_call | solution.py:230
  (16 shorter events, 0.2 us)
Async XLA Ops:
  132.0 5.0 copy-start.3
  132.0 34.4 %all-to-all-start.4 = ((bf16[8,36,8,512]{3,2,1,0:T(8,128)(2,1)}), bf16[8,36,8,512]{3,2,1,0:T(8,128)(2,1)S(1)}, u32[]{:S(2)}, u32[]{:S(2)}) async-start(bf16[8,36,8,512]{3,2,1,0:T(8,128)(2,1)} %get-tuple-element.15), calls=%async_computation.4 | async-start | bytes 4718592 | tf_op jit(solution)/shard_map/all_to_all | solution.py:217
  137.0 134.6 %all-gather.12.cloned.1.call-start = ((), (), s32[]{:S(2)}) async-start(), calls=%async_computation.8 | async-start | bytes 5898240 | tf_op jit(solution)/shard_map/all_gather | solution.py:227
  168.3 175.7 %all-gather.10.cloned.1.call-start = ((), (), s32[]{:S(2)}) async-start(), calls=%async_computation.7 | async-start | bytes 5898240 | tf_op jit(solution)/shard_map/all_gather | solution.py:227
  201.2 1.9 copy-start.1
  203.1 230.3 %all-gather.8.cloned.1.call-start = ((), (), s32[]{:S(2)}) async-start(), calls=%async_computation.6 | async-start | bytes 5898240 | tf_op jit(solution)/shard_map/all_gather | solution.py:227
  235.0 1.9 copy-start
  236.8 285.8 %all-gather.6.cloned.1.call-start = ((), (), s32[]{:S(2)}) async-start(), calls=%async_computation.5 | async-start | bytes 5898240 | tf_op jit(solution)/shard_map/all_gather | solution.py:227
  268.7 1.9 copy-start.2
Sparse Core Ops, SparseCore 0:
  168.4 86.1 all-gather.11
  256.1 87.7 all-gather.9
  345.5 87.7 all-gather.7
  434.8 87.7 all-gather.5
where the time goes:
time: 540 us; the launch traced here: 538 us
  waiting for transfers between devices  255 us (47%)
  blocking collectives  183 us (34%)
  Pallas kernels  71.1 us (13%)
  between operations  15.2 us (3%)
    all_gather x4, waiting for transfers between devices, body(): spread = lax.all_gather(picked, 'dp', axis=1, tiled=True)  225 us
    all_to_all x3, blocking collectives, body(): lax.all_to_all(outs[k], 'shard', split_axis=0, concat_axis=0, tiled=True)  96.6 us
    all_gather x1, blocking collectives, body(): total = lax.all_gather(jnp.sum(pieces, axis=0), ('shard', 'dp'), axis=0)  69.9 us
    pallas_call x4, Pallas kernels, body(): pl.pallas_call(place_kernel, grid=(total_blocks // run,), in_specs=[pl.Bl...  34.3 us
    all_to_all x1, waiting for transfers between devices, body(): lax.all_to_all(outs[k], 'shard', split_axis=0, concat_axis=0, tiled=True)  29.3 us
    all_to_all x1, blocking collectives, body(): lax.all_to_all(pieces, ('shard', 'dp'), split_axis=0, concat_axis=0, tile...  16.4 us
    pallas_call x1, Pallas kernels, body(): pl.pallas_call(functools.partial(update_kernel, group, mats, parts, row_c...  15.8 us
    pallas_call x1, Pallas kernels, body(): pl.pallas_call(functools.partial(sums_kernel, group, mats, piece), grid_s...  13.6 us
  transfers between devices with their start and end apart: 5, of which 4 were waited for; matrix products, arithmetic and copies ran while one was open for 0% of the time, Pallas kernels for 6%

commit v1 on v0

v1 whole, which is shorter than its diff:
```python
import functools

import jax
import jax.numpy as jnp
from jax import lax
from jax.experimental import pallas as pl
from jax.experimental.pallas import tpu as pltpu
from jax.sharding import PartitionSpec as P

D = 4096
FF = 10240
MATS = 3
CHUNK = 8


def slots_per_step(slot_count):
    return max(n for n in range(1, 5) if slot_count % n == 0)


def sums_kernel(group, mats, piece, ints_ref, floats_ref, grad_ref, state_ref, rows_ref, sums_ref, cols_acc, weighted_acc, rows_acc):
    step = pl.program_id(0)
    owned = ints_ref[0]
    beta = floats_ref[0]
    gain = floats_ref[1]
    height, width = grad_ref.shape[1], grad_ref.shape[2]

    @pl.when(step == 0)
    def _():
        cols_acc[...] = jnp.zeros_like(cols_acc)
        weighted_acc[...] = jnp.zeros_like(weighted_acc)
        rows_acc[...] = jnp.zeros_like(rows_acc)

    for j in range(group):
        slot = step * group + j

        @pl.when(slot >= owned)
        def _():
            rows_ref[j] = jnp.zeros_like(rows_ref[j])

        @pl.when(slot < owned)
        def _():
            m = ints_ref[2 + slot]
            squares = grad_ref[j] * grad_ref[j]
            rows = beta * state_ref[j] + gain * jnp.sum(squares, axis=1, keepdims=True)
            rows_ref[j] = rows
            tall = (height // 8, 8, width)
            cols_acc[m] += jnp.sum(squares.reshape(tall), axis=0)
            weighted_acc[m] += jnp.sum((squares * (1.0 / rows)).reshape(tall), axis=0)
            rows_acc[m] += jnp.sum(jnp.broadcast_to(rows, (height, 128)).reshape(height // 8, 8, 128), axis=0)

    @pl.when(step == pl.num_programs(0) - 1)
    def _():
        sums_ref[...] = jnp.zeros_like(sums_ref)
        for m in range(mats):
            sums_ref[m : m + 1, :] = jnp.sum(cols_acc[m], axis=0, keepdims=True)
            sums_ref[mats + m : mats + m + 1, :] = jnp.sum(weighted_acc[m], axis=0, keepdims=True)
            spot = lax.broadcasted_iota(jnp.int32, (1, sums_ref.shape[1]), 1) % piece == m
            part = jnp.sum(rows_acc[m], axis=0, keepdims=True)[:, 0:1]
            sums_ref[2 * mats : 2 * mats + 1, :] += jnp.where(spot, part, 0.0)


def main_kernel(mats, row_counts, ids_ref, spots_ref, floats_ref, sums_ref, state_ref, rows_ref, grad_ref, param_ref, temp_ref, cols_ref, *scratch):
    (grad_buf, param_buf, send_buf, picked, factor, part_in, part_all, total_all) = scratch[:8]
    (load_sem, part_sem, cross_send, cross_recv, line_send, line_recv, own_sem) = scratch[8:15]
    recv_bufs = scratch[15:]
    parts, copies = lax.axis_size("shard"), lax.axis_size("dp")
    me, z = lax.axis_index("shard"), lax.axis_index("dp")
    row_groups, slot_count, _, width = grad_buf.shape
    units = len(recv_bufs)
    cut = width // parts
    col_groups = units // row_groups
    blocks = picked.shape[1]
    beta, rest, rate = floats_ref[0], floats_ref[2], floats_ref[3]

    def wait(ref, sem):
        pltpu.make_async_copy(ref, ref, sem).wait()

    def loads(k):
        rows = pl.ds(k * CHUNK, CHUNK)
        return (
            pltpu.make_async_copy(grad_ref.at[:, rows, :], grad_buf.at[k], load_sem.at[0, k]),
            pltpu.make_async_copy(param_ref.at[:, rows, :], param_buf.at[k], load_sem.at[1, k]),
        )

    def send(src, dst, send_sem, recv_sem, axis, to):
        pltpu.make_async_remote_copy(
            src_ref=src,
            dst_ref=dst,
            send_sem=send_sem,
            recv_sem=recv_sem,
            device_id={axis: to},
            device_id_type=pl.DeviceIdType.MESH,
        ).start()

    for copy in loads(0):
        copy.start()

    barrier = pltpu.get_barrier_semaphore()
    for axis, at, size in (("shard", me, parts), ("dp", z, copies)):
        for step in range(1, size):
            peer = lax.rem(at + step, size)
            pl.semaphore_signal(barrier, inc=1, device_id={axis: peer}, device_id_type=pl.DeviceIdType.MESH)
    pl.semaphore_wait(barrier, parts + copies - 2)

    for step in range(1, parts):
        to = lax.rem(me + step, parts)
        span = pl.ds(pl.multiple_of(to * cut, 128), cut)
        send(sums_ref.at[:, span], part_in.at[me], part_sem.at[0], part_sem.at[1], "shard", to)
    mine = pl.ds(pl.multiple_of(me * cut, 128), cut)
    pltpu.make_async_copy(sums_ref.at[:, mine], part_in.at[me], part_sem.at[1]).start()
    wait(part_in, part_sem.at[1])
    part_all[z] = jnp.sum(part_in[...], axis=0)
    for step in range(1, copies):
        to = lax.rem(z + step, copies)
        send(part_all.at[z], part_all.at[z], part_sem.at[2], part_sem.at[3], "dp", to)
    wait(part_all.at[pl.ds(0, copies - 1)], part_sem.at[3])
    total_all[me] = jnp.sum(part_all[...], axis=0)
    for step in range(1, parts):
        to = lax.rem(me + step, parts)
        send(total_all.at[me], total_all.at[me], part_sem.at[4], part_sem.at[5], "shard", to)
    for k in range(1, row_groups):
        for copy in loads(k):
            copy.start()
    wait(total_all.at[pl.ds(0, parts - 1)], part_sem.at[5])

    for m in range(mats):
        count = row_counts[m]
        square = jnp.zeros((1, 1), jnp.float32)
        for s in range(parts):
            span = slice(s * cut, (s + 1) * cut)
            cols = beta * state_ref[m : m + 1, span] + rest * (total_all[s, m : m + 1, :] / count)
            cols_ref[m : m + 1, span] = cols
            square += jnp.sum(total_all[s, mats + m : mats + m + 1, :] / cols, axis=1, keepdims=True)
        average = total_all[0, 2 * mats : 2 * mats + 1, m : m + 1] / count
        clip = jnp.maximum(1.0, jnp.sqrt(average * square / (count * width)))
        gain = jnp.sqrt(average) * rate / clip
        for s in range(parts):
            span = slice(s * cut, (s + 1) * cut)
            factor[m, :, span] = jnp.broadcast_to(lax.rsqrt(cols_ref[m : m + 1, span]) * gain, (CHUNK, cut))

    def update(k):
        for copy in loads(k):
            copy.wait()
        for c in range(col_groups):
            u = k * col_groups + c

            def slot(j, carry):
                m = ids_ref[j]
                scale = lax.rsqrt(rows_ref[j, k * CHUNK : (k + 1) * CHUNK, :])
                for s in range(parts):
                    span = slice(s * cut + c * 128, s * cut + (c + 1) * 128)
                    new = param_buf[k, j, :, span].astype(jnp.float32) - grad_buf[k, j, :, span] * scale * factor[m, :, span]
                    send_buf[u, s, j] = new.astype(send_buf.dtype)
                return carry

            lax.fori_loop(0, slot_count, slot, 0)
            spot = pl.ds(me * slot_count, slot_count)
            for step in range(1, parts):
                to = lax.rem(me + step, parts)
                send(send_buf.at[u, to], recv_bufs[u].at[spot], cross_send.at[u], cross_recv.at[u], "shard", to)
            pltpu.make_async_copy(send_buf.at[u, me], recv_bufs[u].at[spot], cross_recv.at[u]).start()

    def own(u):
        wait(recv_bufs[u], cross_recv.at[u])

        def pick(b, carry):
            picked[u, b] = recv_bufs[u][spots_ref[b]]
            return carry

        lax.fori_loop(0, blocks, pick, 0, unroll=8)

        @pl.when(z < copies - 1)
        def _():
            send(picked.at[u], temp_ref.at[z, u], line_send.at[0, 0], line_recv.at[0, 0, u], "dp", z + 1)

        @pl.when(z > 0)
        def _():
            send(picked.at[u], temp_ref.at[z, u], line_send.at[1, 0], line_recv.at[1, 0, u], "dp", z - 1)

        pltpu.make_async_copy(picked.at[u], temp_ref.at[z, u], own_sem).start()

    def forward(h, u):
        @pl.when((z >= h) & (z < copies - 1))
        def _():
            block = temp_ref.at[z - h, u]
            wait(block, line_recv.at[0, h - 1, u])
            send(block, block, line_send.at[0, h], line_recv.at[0, h, u], "dp", z + 1)

        @pl.when((z + h < copies) & (z > 0))
        def _():
            block = temp_ref.at[z + h, u]
            wait(block, line_recv.at[1, h - 1, u])
            send(block, block, line_send.at[1, h], line_recv.at[1, h, u], "dp", z - 1)

    early = min(row_groups, 2)
    for k in range(early):
        update(k)
    later = list(range(early, row_groups))
    for i in range(units + copies - 2):
        if i < units:
            own(i)
        if later:
            update(later.pop(0))
        for h in range(1, copies - 1):
            if 0 <= i - h < units:
                forward(h, i - h)

    for h in range(1, copies):
        for u in range(units):
            @pl.when((z >= h) & (z == copies - 1))
            def _():
                wait(temp_ref.at[z - h, u], line_recv.at[0, h - 1, u])

            @pl.when((z + h < copies) & (z == 0))
            def _():
                wait(temp_ref.at[z + h, u], line_recv.at[1, h - 1, u])

    for h in range(copies - 1):
        @pl.when((z >= h) & (z < copies - 1))
        def _():
            wait(temp_ref.at[0], line_send.at[0, h])

        @pl.when((z + h < copies) & (z > 0))
        def _():
            wait(temp_ref.at[0], line_send.at[1, h])

    wait(temp_ref.at[0], own_sem)
    for u in range(units):
        wait(send_buf.at[u, pl.ds(0, parts - 1)], cross_send.at[u])
    wait(part_in.at[pl.ds(0, parts - 1)], part_sem.at[0])
    wait(part_all.at[pl.ds(0, copies - 1)], part_sem.at[2])
    wait(total_all.at[pl.ds(0, parts - 1)], part_sem.at[4])


def place_kernel(in_ref, out_ref):
    copies, row_groups = out_ref.shape[1], out_ref.shape[2]
    col_groups = in_ref.shape[1] // row_groups
    for d in range(copies):
        for k in range(row_groups):
            for c in range(col_groups):
                out_ref[:, d, k, :, c * 128 : (c + 1) * 128] = in_ref[d, k * col_groups + c]


def body(parts, grad, param, row_state, col_state, block_start, block_matrix, step):
    slot_count, height, width = grad.shape
    mats = col_state.shape[0]
    total_blocks = block_matrix.shape[0]
    group = slots_per_step(slot_count)
    steps = slot_count // group
    chunks = height // CHUNK
    cut = width // parts
    row_counts = (float(D), float(D), float(FF))

    shard_index = lax.axis_index("shard")
    block_ends = jnp.concatenate([block_start[1:], jnp.full((1,), total_blocks, jnp.int32)])
    at_shard = jnp.arange(parts, dtype=jnp.int32) == shard_index
    first_block = jnp.sum(jnp.where(at_shard, block_start, 0))
    owned = jnp.sum(jnp.where(at_shard, block_ends - block_start, 0))
    block_index = jnp.arange(total_blocks, dtype=jnp.int32)
    slot_blocks = first_block + jnp.arange(slot_count, dtype=jnp.int32)
    matrix_ids = jnp.sum(
        jnp.where(slot_blocks[:, None] == block_index[None, :], block_matrix[None, :], 0), axis=1
    )
    started = block_start[None, :] <= block_index[:, None]
    owner = jnp.sum(started.astype(jnp.int32), axis=1) - 1
    owner_start = jnp.max(jnp.where(started, block_start[None, :], 0), axis=1)
    slot_of = owner * slot_count + block_index - owner_start
    ints = jnp.concatenate([jnp.stack([owned, (owned - 1) // group]), matrix_ids]).astype(jnp.int32)
    step_value = step[0].astype(jnp.float32)
    beta = 1.0 - step_value ** (-0.8)
    rate = 1.0 / jnp.sqrt(jnp.maximum(step_value, 10000.0))
    floats = jnp.stack([beta, (1.0 - beta) / width, 1.0 - beta, rate])

    smem = pl.BlockSpec(memory_space=pltpu.SMEM)

    def live(i, ints_ref):
        return jnp.minimum(i, ints_ref[1])

    new_rows, sums = pl.pallas_call(
        functools.partial(sums_kernel, group, mats, cut),
        grid_spec=pltpu.PrefetchScalarGridSpec(
            num_scalar_prefetch=1,
            grid=(steps,),
            in_specs=[
                smem,
                pl.BlockSpec((group, height, width), lambda i, s: (live(i, s), 0, 0)),
                pl.BlockSpec((group, height, 1), lambda i, s: (i, 0, 0)),
            ],
            out_specs=[
                pl.BlockSpec((group, height, 1), lambda i, s: (i, 0, 0)),
                pl.BlockSpec((8, width), lambda i, s: (0, 0)),
            ],
            scratch_shapes=[
                pltpu.VMEM((mats, 8, width), jnp.float32),
                pltpu.VMEM((mats, 8, width), jnp.float32),
                pltpu.VMEM((mats, 8, 128), jnp.float32),
            ],
        ),
        out_shape=[
            jax.ShapeDtypeStruct((slot_count, height, 1), jnp.float32),
            jax.ShapeDtypeStruct((8, width), jnp.float32),
        ],
        compiler_params=pltpu.CompilerParams(vmem_limit_bytes=60 * 2**20),
        cost_estimate=pl.CostEstimate(flops=grad.size * 6, bytes_accessed=grad.size * 4, transcendentals=0),
        name="sums",
    )(ints, floats, grad, row_state[:, :, None])

    copies = lax.axis_size("dp")
    units = chunks * (cut // 128)
    vmem = pl.BlockSpec(memory_space=pltpu.VMEM)
    hbm = pl.BlockSpec(memory_space=pl.ANY)
    dma = pltpu.SemaphoreType.DMA
    temp, new_cols = pl.pallas_call(
        functools.partial(main_kernel, mats, row_counts),
        in_specs=[smem, smem, smem, vmem, vmem, vmem, hbm, hbm],
        out_specs=[hbm, vmem],
        out_shape=[
            jax.ShapeDtypeStruct((copies, units, total_blocks, CHUNK, 128), jnp.bfloat16),
            jax.ShapeDtypeStruct((mats, width), jnp.float32),
        ],
        scratch_shapes=[
            pltpu.VMEM((chunks, slot_count, CHUNK, width), jnp.float32),
            pltpu.VMEM((chunks, slot_count, CHUNK, width), jnp.bfloat16),
            pltpu.VMEM((units, parts, slot_count, CHUNK, 128), jnp.bfloat16),
            pltpu.VMEM((units, total_blocks, CHUNK, 128), jnp.bfloat16),
            pltpu.VMEM((mats, CHUNK, width), jnp.float32),
            pltpu.VMEM((parts, 8, cut), jnp.float32),
            pltpu.VMEM((copies, 8, cut), jnp.float32),
            pltpu.VMEM((parts, 8, cut), jnp.float32),
            dma((2, chunks)),
            dma((6,)),
            dma((units,)),
            dma((units,)),
            dma((2, copies - 1)),
            dma((2, copies - 1, units)),
            dma(()),
        ]
        + [pltpu.VMEM((parts * slot_count, CHUNK, 128), jnp.bfloat16) for _ in range(units)],
        compiler_params=pltpu.CompilerParams(
            collective_id=0, has_side_effects=True, vmem_limit_bytes=63 * 2**20
        ),
        cost_estimate=pl.CostEstimate(flops=grad.size * 6, bytes_accessed=grad.size * 8, transcendentals=0),
        name="main",
    )(matrix_ids, slot_of, floats, sums, col_state, new_rows, grad, param)

    run = 12 if total_blocks % 12 == 0 else 1
    placed = pl.pallas_call(
        place_kernel,
        grid=(total_blocks // run,),
        in_specs=[pl.BlockSpec((copies, units, run, CHUNK, 128), lambda i: (0, 0, i, 0, 0))],
        out_specs=pl.BlockSpec((run, copies, chunks, CHUNK, cut), lambda i: (i, 0, 0, 0, 0)),
        out_shape=jax.ShapeDtypeStruct((total_blocks, copies, chunks, CHUNK, cut), jnp.bfloat16),
        compiler_params=pltpu.CompilerParams(vmem_limit_bytes=60 * 2**20),
        cost_estimate=pl.CostEstimate(flops=0, bytes_accessed=2 * total_blocks * copies * height * cut * 2, transcendentals=0),
        name="place",
    )(temp)
    new_params = placed.reshape(total_blocks * copies * height, cut)
    return new_params, new_rows[:, :, 0], new_cols


def solution(mesh):
    return jax.shard_map(
        functools.partial(body, mesh.shape["shard"]),
        mesh=mesh,
        in_specs=(
            P("shard", "dp", None),
            P("shard", "dp", None),
            P("shard", "dp"),
            P(),
            P(),
            P(),
            P(),
        ),
        out_specs=(P(None, "shard"), P("shard", "dp"), P()),
        check_vma=False,
    )
```

time: 540 us -> 408 us (0.76)
  Pallas kernels: 71.1 us -> 393 us
  waiting for transfers between devices: 255 us -> 0 us
  blocking collectives: 183 us -> 0 us
  between operations: 15.2 us -> 2.08 us
    pallas_call x6 -> x2, Pallas kernels: 36.8 us -> 375 us  [the longest x1 363 us: body(): pl.pallas_call(functools.partial(main_kernel, mats, row_counts), in_specs...]
    all_gather x4 -> x0, waiting for transfers between devices: 225 us -> none  [body(): spread = lax.all_gather(picked, 'dp', axis=1, tiled=True)]
    all_to_all x4 -> x0, blocking collectives: 113 us -> none  [the longest x3 96.6 us: body(): lax.all_to_all(outs[k], 'shard', split_axis=0, concat_axis=0, tiled=True)]
    all_gather x1 -> x0, blocking collectives: 69.9 us -> none  [body(): total = lax.all_gather(jnp.sum(pieces, axis=0), ('shard', 'dp'), axis=0)]
    all_to_all x1 -> x0, waiting for transfers between devices: 29.3 us -> none  [body(): lax.all_to_all(outs[k], 'shard', split_axis=0, concat_axis=0, tiled=True)]
    pallas_call x4 -> x1, Pallas kernels: 34.3 us -> 18.3 us  [body(): pl.pallas_call(place_kernel, grid=(total_blocks // run,), in_specs=[pl.Bl...]
  transfers between devices with their start and end apart: 5 -> 0, of which waited for: 4 -> 0; matrix products, arithmetic and copies ran while one was open for 0% -> 0% of each run, Pallas kernels for 6% -> 0%
where the time goes in v1:
time: 408 us; the launch traced here: 407 us
  Pallas kernels  393 us (96%)
  other arithmetic  6.14 us (2%)
  local copies, waits for them, and re-layouts  5.51 us (1%)
    pallas_call x1, Pallas kernels, body(): pl.pallas_call(functools.partial(main_kernel, mats, row_counts), in_specs...  363 us
    pallas_call x1, Pallas kernels, body(): pl.pallas_call(place_kernel, grid=(total_blocks // run,), in_specs=[pl.Bl...  18.3 us
    pallas_call x1, Pallas kernels, body(): pl.pallas_call(functools.partial(sums_kernel, group, mats, cut), grid_spe...  11.6 us

profile of v1, /device:TPU:0, one launch (start us, length us, event | category | flops | bytes accessed | tf_op | source)
XLA Modules:
  0.0 406.8 jit_solution(10846256406793194790)
XLA Ops:
  1.4 0.7 pad_maximum_fusion.floats_ref
  2.0 0.7 slice.3
  2.8 1.4 fusion.1
  4.8 0.7 iota_add_fusion
  5.4 0.9 select_reduce_fusion.ids_ref
  6.3 0.0 copy-start.1
  6.3 1.3 pad_add_fusion.ints_ref
  7.6 0.7 convert_reduce_fusion
  8.4 0.6 add_subtract_fusion.spots_ref
  8.9 2.1 copy.14.state_ref
  11.0 11.6 %sums.1 = (f32[36,32,1]{2,1,0:T(8,128)}, f32[8,4096]{1,0:T(8,128)}) custom-call(s32[38]{0:T(128)} %pad_add_fusion.ints_ref, f32[4]{0:T(128)} %pad_maximum_fusion.floats_ref, f32[36,32,4096]{2,1,0:T(8,128)} %grad_ref.3, f32[36,32,1]{2,1,0:T(8,128)} %copy.14.state_ref), custom_call_target="tpu_custom_call" | custom-call | flops 28311552 | bytes 18874368 | tf_op jit(solution)/shard_map/sums/pallas_call | solution.py:279
  22.6 2.1 copy.15
  24.6 0.0 copy-done.1
  24.6 363.2 %main.1 = (bf16[4,16,144,8,128]{4,3,2,1,0:T(8,128)(2,1)}, f32[3,4096]{1,0:T(4,128)}) custom-call(s32[36]{0:T(128)} %copy-done.1, s32[144]{0:T(256)} %add_subtract_fusion.spots_ref, f32[4]{0:T(128)} %pad_maximum_fusion.floats_ref, f32[8,4096]{1,0:T(8,128)} %get-tuple-element.7.sums_ref, f32[3,4096]{1,0:T(4,128)} %state_ref.1, ...), custom_call_target="tpu_custom_call" | custom-call | flops 28311552 | bytes 37748736 | tf_op jit(solution)/shard_map/main/pallas_call | solution.py:313
  387.9 0.0 copy-start
  387.9 18.3 %place.1 = bf16[144,4,4,8,512]{4,3,2,1,0:T(8,128)(2,1)} custom-call(bf16[4,16,144,8,128]{4,3,2,1,0:T(8,128)(2,1)} %get-tuple-element.9.in_ref), custom_call_target="tpu_custom_call" | custom-call | bytes 37748736 | tf_op jit(solution)/shard_map/place/pallas_call | solution.py:347
  406.1 0.0 copy-done
  406.1 0.6 copy.18
Async XLA Ops:
  6.3 18.3 %copy-start.1 = (s32[36]{0:T(128)}, s32[36]{0:T(128)S(1)}, u32[]{:S(2)}) copy-start(s32[36]{0:T(128)S(1)} %select_reduce_fusion.ids_ref) | copy-start | bytes 436
  387.9 18.3 %copy-start = (f32[3,4096]{1,0:T(4,128)S(1)}, f32[3,4096]{1,0:T(4,128)}, u32[]{:S(2)}) copy-start(f32[3,4096]{1,0:T(4,128)} %get-tuple-element.23) | copy-start | bytes 147460

commit v2 on v1

v2 whole, which is shorter than its diff:
```python
import functools

import jax
import jax.numpy as jnp
from jax import lax
from jax.experimental import pallas as pl
from jax.experimental.pallas import tpu as pltpu
from jax.sharding import PartitionSpec as P

D = 4096
FF = 10240
MATS = 3
CHUNK = 8


def largest(limit, count):
    return max(n for n in range(1, limit + 1) if count % n == 0)


def wait(ref, sem):
    pltpu.make_async_copy(ref, ref, sem).wait()


def first_and_owned(start_ref, blocks):
    parts = start_ref.shape[0]
    me = lax.axis_index("shard")
    first = start_ref[me]
    end = jnp.where(me == parts - 1, blocks, start_ref[jnp.minimum(me + 1, parts - 1)])
    return first, end - first


def decay_of(step_ref, shape):
    return jnp.exp(-0.8 * jnp.log(jnp.full(shape, step_ref[0], jnp.int32).astype(jnp.float32)))


def sums_kernel(group, mats, cut, start_ref, matrix_ref, step_ref, grad_ref, state_ref, rows_ref, scale_ref, sums_ref, cols_acc, weighted_acc, rows_acc):
    i = pl.program_id(0)
    blocks = matrix_ref.shape[0]
    first, owned = first_and_owned(start_ref, blocks)
    height, width = grad_ref.shape[1], grad_ref.shape[2]
    spans = [slice(n, n + 128) for n in range(0, width, 128)]

    def fold(tile):
        parts = [tile[n : n + 8] for n in range(0, height, 8)]
        while len(parts) > 1:
            parts = [a + b for a, b in zip(parts[::2], parts[1::2])] + parts[len(parts) & ~1 :]
        return parts[0]

    @pl.when(i == 0)
    def _():
        rows_ref[...] = jnp.zeros_like(rows_ref)
        cols_acc[...] = jnp.zeros_like(cols_acc)
        weighted_acc[...] = jnp.zeros_like(weighted_acc)
        rows_acc[...] = jnp.zeros_like(rows_acc)

    @pl.when(i * group < owned)
    def _():
        decay = decay_of(step_ref, (height, 1))
        eye = lax.broadcasted_iota(jnp.int32, (height, height), 0) == lax.broadcasted_iota(jnp.int32, (height, height), 1)
        work = []
        for j in range(group):
            slot = i * group + j
            live = slot < owned
            m = jnp.where(live, matrix_ref[jnp.minimum(first + slot, blocks - 1)], mats)
            across = jnp.zeros((height, 128), jnp.float32)
            for span in spans:
                tile = grad_ref[j, :, span]
                tile = tile * tile
                across += tile
                cols_acc[m, :, span] += fold(tile)
            state = jnp.sum(jnp.where(eye, state_ref[pl.ds(slot, 1), :], 0.0), axis=1, keepdims=True)
            total = jnp.sum(across, axis=1, keepdims=True)
            rows = (1.0 - decay) * state + decay * (total / width)
            flat = jnp.sum(jnp.where(eye, rows, 0.0), axis=0, keepdims=True)
            rows_ref[pl.ds(slot, 1), :] = jnp.where(live, flat, 0.0)
            rows = jnp.broadcast_to(rows, (height, 128))
            scale_ref[j] = lax.rsqrt(rows)
            rows_acc[m] += fold(rows)
            work.append((j, m, 1.0 / rows))
        for j, m, inverse in work:
            for span in spans:
                tile = grad_ref[j, :, span]
                weighted_acc[m, :, span] += fold(tile * tile * inverse)

    @pl.when(i == pl.num_programs(0) - 1)
    def _():
        sums_ref[...] = jnp.zeros_like(sums_ref)
        for m in range(mats):
            sums_ref[m : m + 1, :] = jnp.sum(cols_acc[m], axis=0, keepdims=True)
            sums_ref[mats + m : mats + m + 1, :] = jnp.sum(weighted_acc[m], axis=0, keepdims=True)
            spot = lax.broadcasted_iota(jnp.int32, (1, width), 1) % cut == m
            part = jnp.sum(rows_acc[m], axis=0, keepdims=True)[:, 0:1]
            sums_ref[2 * mats : 2 * mats + 1, :] += jnp.where(spot, part, 0.0)


def main_kernel(mats, row_counts, start_ref, matrix_ref, step_ref, sums_ref, state_ref, scale_ref, grad_ref, param_ref, temp_ref, cols_ref, *scratch):
    (ids, spots, grad_buf, param_buf, scale_buf, send_buf, picked, factor, part_in, part_all, total_all) = scratch[:11]
    (load_sem, part_sem, cross_send, cross_recv, line_send, line_recv, own_sem) = scratch[11:18]
    recv_bufs = scratch[18:]
    parts, copies = lax.axis_size("shard"), lax.axis_size("dp")
    me, z = lax.axis_index("shard"), lax.axis_index("dp")
    row_groups, slot_count, _, width = grad_buf.shape
    units = len(recv_bufs)
    cut = width // parts
    col_groups = units // row_groups
    blocks = picked.shape[1]
    def loads(k):
        rows = pl.ds(k * CHUNK, CHUNK)
        return (
            pltpu.make_async_copy(grad_ref.at[:, rows, :], grad_buf.at[k], load_sem.at[0, k]),
            pltpu.make_async_copy(param_ref.at[:, rows, :], param_buf.at[k], load_sem.at[1, k]),
            pltpu.make_async_copy(scale_ref.at[:, rows, :], scale_buf.at[k], load_sem.at[2, k]),
        )

    def send(src, dst, send_sem, recv_sem, axis, to):
        pltpu.make_async_remote_copy(
            src_ref=src,
            dst_ref=dst,
            send_sem=send_sem,
            recv_sem=recv_sem,
            device_id={axis: to},
            device_id_type=pl.DeviceIdType.MESH,
        ).start()

    for copy in loads(0):
        copy.start()

    barrier = pltpu.get_barrier_semaphore()
    for axis, at, size in (("shard", me, parts), ("dp", z, copies)):
        for step in range(1, size):
            peer = lax.rem(at + step, size)
            pl.semaphore_signal(barrier, inc=1, device_id={axis: peer}, device_id_type=pl.DeviceIdType.MESH)

    first = start_ref[me]

    def note_id(j, carry):
        ids[j] = matrix_ref[jnp.minimum(first + j, blocks - 1)]
        return carry

    def note_spot(b, carry):
        shift = jnp.int32(0)
        for s in range(1, parts):
            shift = jnp.where(b >= start_ref[s], s * slot_count - start_ref[s], shift)
        spots[b] = jnp.minimum(b + shift, parts * slot_count - 1)
        return carry

    lax.fori_loop(0, slot_count, note_id, 0)
    lax.fori_loop(0, blocks, note_spot, 0)
    pl.semaphore_wait(barrier, parts + copies - 2)

    for step in range(1, parts):
        to = lax.rem(me + step, parts)
        span = pl.ds(pl.multiple_of(to * cut, 128), cut)
        send(sums_ref.at[:, span], part_in.at[me], part_sem.at[0], part_sem.at[1], "shard", to)
    mine = pl.ds(pl.multiple_of(me * cut, 128), cut)
    pltpu.make_async_copy(sums_ref.at[:, mine], part_in.at[me], part_sem.at[1]).start()
    wait(part_in, part_sem.at[1])
    part_all[z] = jnp.sum(part_in[...], axis=0)
    for step in range(1, copies):
        to = lax.rem(z + step, copies)
        send(part_all.at[z], part_all.at[z], part_sem.at[2], part_sem.at[3], "dp", to)
    wait(part_all.at[pl.ds(0, copies - 1)], part_sem.at[3])
    total_all[me] = jnp.sum(part_all[...], axis=0)
    for step in range(1, parts):
        to = lax.rem(me + step, parts)
        send(total_all.at[me], total_all.at[me], part_sem.at[4], part_sem.at[5], "shard", to)
    for k in range(1, row_groups):
        for copy in loads(k):
            copy.start()
    wait(total_all.at[pl.ds(0, parts - 1)], part_sem.at[5])

    decay = decay_of(step_ref, (1, 1))
    step = jnp.full((1, 1), step_ref[0], jnp.int32).astype(jnp.float32)
    rate = 1.0 / jnp.sqrt(jnp.maximum(step, 10000.0))
    for m in range(mats):
        count = row_counts[m]
        square = jnp.zeros((1, 1), jnp.float32)
        for s in range(parts):
            span = slice(s * cut, (s + 1) * cut)
            cols = (1.0 - decay) * state_ref[m : m + 1, span] + decay * (total_all[s, m : m + 1, :] / count)
            cols_ref[m : m + 1, span] = cols
            square += jnp.sum(total_all[s, mats + m : mats + m + 1, :] / cols, axis=1, keepdims=True)
        average = total_all[0, 2 * mats : 2 * mats + 1, m : m + 1] / count
        clip = jnp.maximum(1.0, jnp.sqrt(average * square / (count * width)))
        gain = jnp.sqrt(average) * rate / clip
        for s in range(parts):
            span = slice(s * cut, (s + 1) * cut)
            factor[m, :, span] = jnp.broadcast_to(lax.rsqrt(cols_ref[m : m + 1, span]) * gain, (CHUNK, cut))

    unroll = largest(4, slot_count)

    def update(u):
        k, c = u // col_groups, u % col_groups
        if c == 0:
            for copy in loads(k):
                copy.wait()

        def slot(j, carry):
            m = ids[j]
            scale = scale_buf[k, j]
            for s in range(parts):
                span = slice(s * cut + c * 128, s * cut + (c + 1) * 128)
                new = param_buf[k, j, :, span].astype(jnp.float32) - grad_buf[k, j, :, span] * scale * factor[m, :, span]
                send_buf[u, s, j] = new.astype(send_buf.dtype)
            return carry

        lax.fori_loop(0, slot_count, slot, 0, unroll=unroll)
        spot = pl.ds(me * slot_count, slot_count)
        for step in range(1, parts):
            to = lax.rem(me + step, parts)
            send(send_buf.at[u, to], recv_bufs[u].at[spot], cross_send.at[u], cross_recv.at[u], "shard", to)
        pltpu.make_async_copy(send_buf.at[u, me], recv_bufs[u].at[spot], cross_recv.at[u]).start()

    def own(u):
        wait(recv_bufs[u], cross_recv.at[u])

        def pick(b, carry):
            picked[u, b] = recv_bufs[u][spots[b]]
            return carry

        lax.fori_loop(0, blocks, pick, 0, unroll=8)

        @pl.when(z < copies - 1)
        def _():
            send(picked.at[u], temp_ref.at[z, u], line_send.at[0, 0], line_recv.at[0, 0, u], "dp", z + 1)

        @pl.when(z > 0)
        def _():
            send(picked.at[u], temp_ref.at[z, u], line_send.at[1, 0], line_recv.at[1, 0, u], "dp", z - 1)

        pltpu.make_async_copy(picked.at[u], temp_ref.at[z, u], own_sem).start()

    def forward(h, u):
        @pl.when((z >= h) & (z < copies - 1))
        def _():
            block = temp_ref.at[z - h, u]
            wait(block, line_recv.at[0, h - 1, u])
            send(block, block, line_send.at[0, h], line_recv.at[0, h, u], "dp", z + 1)

        @pl.when((z + h < copies) & (z > 0))
        def _():
            block = temp_ref.at[z + h, u]
            wait(block, line_recv.at[1, h - 1, u])
            send(block, block, line_send.at[1, h], line_recv.at[1, h, u], "dp", z - 1)

    early = min(units, 8)
    for u in range(early):
        update(u)
    later = list(range(early, units))
    for i in range(units + copies - 2):
        if i < units:
            own(i)
        for u in later[:4]:
            update(u)
        later = later[4:]
        for h in range(1, copies - 1):
            if 0 <= i - h < units:
                forward(h, i - h)

    for h in range(1, copies):
        for u in range(units):
            @pl.when((z >= h) & (z == copies - 1))
            def _():
                wait(temp_ref.at[z - h, u], line_recv.at[0, h - 1, u])

            @pl.when((z + h < copies) & (z == 0))
            def _():
                wait(temp_ref.at[z + h, u], line_recv.at[1, h - 1, u])

    for h in range(copies - 1):
        @pl.when((z >= h) & (z < copies - 1))
        def _():
            wait(temp_ref.at[0], line_send.at[0, h])

        @pl.when((z + h < copies) & (z > 0))
        def _():
            wait(temp_ref.at[0], line_send.at[1, h])

    wait(temp_ref.at[0], own_sem)
    for u in range(units):
        wait(send_buf.at[u, pl.ds(0, parts - 1)], cross_send.at[u])
    wait(part_in.at[pl.ds(0, parts - 1)], part_sem.at[0])
    wait(part_all.at[pl.ds(0, copies - 1)], part_sem.at[2])
    wait(total_all.at[pl.ds(0, parts - 1)], part_sem.at[4])


def place_kernel(in_ref, out_ref, buf, load_sem, store_sem):
    copies, row_groups = buf.shape[0], buf.shape[1]
    col_groups = in_ref.shape[1] // row_groups
    where = [(d, k) for d in range(copies) for k in range(row_groups)]
    for d, k in where:
        for c in range(col_groups):
            span = slice(c * 128, (c + 1) * 128)
            pltpu.make_async_copy(in_ref.at[d, k * col_groups + c], buf.at[d, k, :, :, span], load_sem.at[d, k]).start()
    for d, k in where:
        wait(buf.at[d, k], load_sem.at[d, k])
        pltpu.make_async_copy(buf.at[d, k], out_ref.at[:, d, k], store_sem).start()
    wait(buf, store_sem)


def body(parts, grad, param, row_state, col_state, block_start, block_matrix, step):
    slot_count, height, width = grad.shape
    mats = col_state.shape[0]
    total_blocks = block_matrix.shape[0]
    group = largest(4, slot_count)
    steps = slot_count // group
    chunks = height // CHUNK
    cut = width // parts
    copies = lax.axis_size("dp")
    units = chunks * (cut // 128)
    row_counts = (float(D), float(D), float(FF))

    smem = pl.BlockSpec(memory_space=pltpu.SMEM)
    vmem = pl.BlockSpec(memory_space=pltpu.VMEM)
    hbm = pl.BlockSpec(memory_space=pl.ANY)
    dma = pltpu.SemaphoreType.DMA

    def live(i, start_ref):
        owned = first_and_owned(start_ref, total_blocks)[1]
        return jnp.minimum(i, (owned - 1) // group)

    new_rows, scale, sums = pl.pallas_call(
        functools.partial(sums_kernel, group, mats, cut),
        grid_spec=pltpu.PrefetchScalarGridSpec(
            num_scalar_prefetch=3,
            grid=(steps,),
            in_specs=[
                pl.BlockSpec((group, height, width), lambda i, s, b, t: (live(i, s), 0, 0)),
                pl.BlockSpec((slot_count, height), lambda i, s, b, t: (0, 0)),
            ],
            out_specs=[
                pl.BlockSpec((slot_count, height), lambda i, s, b, t: (0, 0)),
                pl.BlockSpec((group, height, 128), lambda i, s, b, t: (live(i, s), 0, 0)),
                pl.BlockSpec((8, width), lambda i, s, b, t: (0, 0)),
            ],
            scratch_shapes=[
                pltpu.VMEM((mats + 1, 8, width), jnp.float32),
                pltpu.VMEM((mats + 1, 8, width), jnp.float32),
                pltpu.VMEM((mats + 1, 8, 128), jnp.float32),
            ],
        ),
        out_shape=[
            jax.ShapeDtypeStruct((slot_count, height), jnp.float32),
            jax.ShapeDtypeStruct((slot_count, height, 128), jnp.float32),
            jax.ShapeDtypeStruct((8, width), jnp.float32),
        ],
        compiler_params=pltpu.CompilerParams(vmem_limit_bytes=60 * 2**20),
        cost_estimate=pl.CostEstimate(flops=grad.size * 6, bytes_accessed=grad.size * 4, transcendentals=0),
        name="sums",
    )(block_start, block_matrix, step, grad, row_state)

    temp, new_cols = pl.pallas_call(
        functools.partial(main_kernel, mats, row_counts),
        in_specs=[smem, smem, smem, vmem, vmem, hbm, hbm, hbm],
        out_specs=[hbm, vmem],
        out_shape=[
            jax.ShapeDtypeStruct((copies, units, total_blocks, CHUNK, 128), jnp.bfloat16),
            jax.ShapeDtypeStruct((mats, width), jnp.float32),
        ],
        scratch_shapes=[
            pltpu.SMEM((slot_count,), jnp.int32),
            pltpu.SMEM((total_blocks,), jnp.int32),
            pltpu.VMEM((chunks, slot_count, CHUNK, width), jnp.float32),
            pltpu.VMEM((chunks, slot_count, CHUNK, width), jnp.bfloat16),
            pltpu.VMEM((chunks, slot_count, CHUNK, 128), jnp.float32),
            pltpu.VMEM((units, parts, slot_count, CHUNK, 128), jnp.bfloat16),
            pltpu.VMEM((units, total_blocks, CHUNK, 128), jnp.bfloat16),
            pltpu.VMEM((mats, CHUNK, width), jnp.float32),
            pltpu.VMEM((parts, 8, cut), jnp.float32),
            pltpu.VMEM((copies, 8, cut), jnp.float32),
            pltpu.VMEM((parts, 8, cut), jnp.float32),
            dma((3, chunks)),
            dma((6,)),
            dma((units,)),
            dma((units,)),
            dma((2, copies - 1)),
            dma((2, copies - 1, units)),
            dma(()),
        ]
        + [pltpu.VMEM((parts * slot_count, CHUNK, 128), jnp.bfloat16) for _ in range(units)],
        compiler_params=pltpu.CompilerParams(
            collective_id=0, has_side_effects=True, vmem_limit_bytes=63 * 2**20
        ),
        cost_estimate=pl.CostEstimate(flops=grad.size * 6, bytes_accessed=grad.size * 8, transcendentals=0),
        name="main",
    )(block_start, block_matrix, step, sums, col_state, scale, grad, param)

    placed = pl.pallas_call(
        place_kernel,
        in_specs=[hbm],
        out_specs=hbm,
        out_shape=jax.ShapeDtypeStruct((total_blocks, copies, chunks, CHUNK, cut), jnp.bfloat16),
        scratch_shapes=[
            pltpu.VMEM((copies, chunks, total_blocks, CHUNK, cut), jnp.bfloat16),
            dma((copies, chunks)),
            dma(()),
        ],
        compiler_params=pltpu.CompilerParams(vmem_limit_bytes=60 * 2**20),
        cost_estimate=pl.CostEstimate(flops=0, bytes_accessed=2 * total_blocks * copies * height * cut * 2, transcendentals=0),
        name="place",
    )(temp)
    new_params = placed.reshape(total_blocks * copies * height, cut)
    return new_params, new_rows, new_cols


def solution(mesh):
    return jax.shard_map(
        functools.partial(body, mesh.shape["shard"]),
        mesh=mesh,
        in_specs=(
            P("shard", "dp", None),
            P("shard", "dp", None),
            P("shard", "dp"),
            P(),
            P(),
            P(),
            P(),
        ),
        out_specs=(P(None, "shard"), P("shard", "dp"), P()),
        check_vma=False,
    )
```

time: 408 us -> 364 us (0.89)
  Pallas kernels: 393 us -> 358 us
  other arithmetic: 6.14 us -> 0 us
    pallas_call x1, Pallas kernels: 363 us -> 333 us  [body(): pl.pallas_call(functools.partial(main_kernel, mats, row_counts), in_specs...]
    pallas_call x1, Pallas kernels: 18.3 us -> 13.3 us  [body(): pl.pallas_call(place_kernel, in_specs=[hbm], out_specs=hbm, out_shape=jax...]
where the time goes in v2:
time: 364 us; the launch traced here: 362 us
  Pallas kernels  358 us (98%)
    pallas_call x1, Pallas kernels, body(): pl.pallas_call(functools.partial(main_kernel, mats, row_counts), in_specs...  333 us
    pallas_call x1, Pallas kernels, body(): pl.pallas_call(place_kernel, in_specs=[hbm], out_specs=hbm, out_shape=jax...  13.3 us
    pallas_call x1, Pallas kernels, body(): pl.pallas_call(functools.partial(sums_kernel, group, mats, cut), grid_spe...  10.9 us

profile of v2, /device:TPU:0, one launch (start us, length us, event | category | flops | bytes accessed | tf_op | source)
XLA Modules:
  0.0 362.3 jit_solution(3747965087440527271)
XLA Ops:
  1.3 1.4 copy.10.state_ref
  2.7 10.9 %sums.1 = (f32[36,32]{1,0:T(8,128)}, f32[36,32,128]{2,1,0:T(8,128)}, f32[8,4096]{1,0:T(8,128)}) custom-call(s32[8]{0:T(128)} %start_ref.3, s32[144]{0:T(256)} %matrix_ref.3, s32[1]{0:T(128)S(6)} %copy.13.step_ref, f32[36,32,4096]{2,1,0:T(8,128)} %grad_ref.3, f32[36,32]{1,0:T(8,128)} %copy.10.state_ref), custom_call_target="tpu_custom_call" | custom-call | flops 28311552 | bytes 18874368 | tf_op jit(solution)/shard_map/sums/pallas_call | solution.py:322
  13.6 1.4 copy.11
  15.0 333.4 %main.1 = (bf16[4,16,144,8,128]{4,3,2,1,0:T(8,128)(2,1)}, f32[3,4096]{1,0:T(4,128)}) custom-call(s32[8]{0:T(128)} %start_ref.3, s32[144]{0:T(256)} %matrix_ref.3, s32[1]{0:T(128)S(6)} %copy.13.step_ref, f32[8,4096]{1,0:T(8,128)} %get-tuple-element.8.sums_ref, f32[3,4096]{1,0:T(4,128)} %state_ref.2, f32[36,32,128]{2,1,0:T(8,128)} %get-tuple-element.9.scale_ref, ...), custom_call_target="tpu_custom_call" | custom-call | flops 28311552 | bytes 37748736 | tf_op jit(solution)/shard_map/main/pallas_call | solution.py:352
  348.4 0.0 copy-start
  348.4 13.3 %place.1 = bf16[144,4,4,8,512]{4,3,2,1,0:T(8,128)(2,1)} custom-call(bf16[4,16,144,8,128]{4,3,2,1,0:T(8,128)(2,1)} %get-tuple-element.10.in_ref), custom_call_target="tpu_custom_call" | custom-call | bytes 37748736 | tf_op jit(solution)/shard_map/place/pallas_call | solution.py:388
  361.7 0.0 copy-done
  361.7 0.6 copy.14
Async XLA Ops:
  348.4 13.3 %copy-start = (f32[3,4096]{1,0:T(4,128)S(1)}, f32[3,4096]{1,0:T(4,128)}, u32[]{:S(2)}) copy-start(f32[3,4096]{1,0:T(4,128)} %get-tuple-element.21) | copy-start | bytes 147460

commit v3 on v2

--- a/solution.py
+++ b/solution.py
@@ -33,12 +33,26 @@
     return jnp.exp(-0.8 * jnp.log(jnp.full(shape, step_ref[0], jnp.int32).astype(jnp.float32)))
 
 
-def sums_kernel(group, mats, cut, start_ref, matrix_ref, step_ref, grad_ref, state_ref, rows_ref, scale_ref, sums_ref, cols_acc, weighted_acc, rows_acc):
-    i = pl.program_id(0)
+def sums_kernel(group, mats, cut, start_ref, matrix_ref, step_ref, state_ref, grad_ref, rows_ref, sums_ref, scale_ref, grad_buf, scale_buf, cols_acc, weighted_acc, rows_acc, load_sem, store_sem):
     blocks = matrix_ref.shape[0]
     first, owned = first_and_owned(start_ref, blocks)
+    groups = (owned + group - 1) // group
     height, width = grad_ref.shape[1], grad_ref.shape[2]
     spans = [slice(n, n + 128) for n in range(0, width, 128)]
+
+    def load(i):
+        slots = pl.ds(i * group, group)
+        return pltpu.make_async_copy(grad_ref.at[slots], grad_buf.at[slots], load_sem.at[i])
+
+    def store(i):
+        slots = pl.ds(i * group, group)
+        return pltpu.make_async_copy(scale_buf.at[slots], scale_ref.at[slots], store_sem.at[i])
+
+    def start_load(i, carry):
+        load(i).start()
+        return carry
+
+    lax.fori_loop(0, groups, start_load, 0)
 
     def fold(tile):
         parts = [tile[n : n + 8] for n in range(0, height, 8)]
@@ -46,57 +60,62 @@
             parts = [a + b for a, b in zip(parts[::2], parts[1::2])] + parts[len(parts) & ~1 :]
         return parts[0]
 
-    @pl.when(i == 0)
-    def _():
-        rows_ref[...] = jnp.zeros_like(rows_ref)
-        cols_acc[...] = jnp.zeros_like(cols_acc)
-        weighted_acc[...] = jnp.zeros_like(weighted_acc)
-        rows_acc[...] = jnp.zeros_like(rows_acc)
-
-    @pl.when(i * group < owned)
-    def _():
-        decay = decay_of(step_ref, (height, 1))
-        eye = lax.broadcasted_iota(jnp.int32, (height, height), 0) == lax.broadcasted_iota(jnp.int32, (height, height), 1)
-        work = []
+    rows_ref[...] = jnp.zeros_like(rows_ref)
+    cols_acc[...] = jnp.zeros_like(cols_acc)
+    weighted_acc[...] = jnp.zeros_like(weighted_acc)
+    rows_acc[...] = jnp.zeros_like(rows_acc)
+    decay = decay_of(step_ref, (height, 1))
+    lane = lax.broadcasted_iota(jnp.int32, rows_ref.shape, 1)
+
+    def work(i, carry):
+        load(i).wait()
+        inverses = []
         for j in range(group):
             slot = i * group + j
             live = slot < owned
             m = jnp.where(live, matrix_ref[jnp.minimum(first + slot, blocks - 1)], mats)
             across = jnp.zeros((height, 128), jnp.float32)
             for span in spans:
-                tile = grad_ref[j, :, span]
+                tile = grad_buf[slot, :, span]
                 tile = tile * tile
                 across += tile
                 cols_acc[m, :, span] += fold(tile)
-            state = jnp.sum(jnp.where(eye, state_ref[pl.ds(slot, 1), :], 0.0), axis=1, keepdims=True)
+            state = jnp.sum(jnp.where(lane == slot, state_ref[...], 0.0), axis=1, keepdims=True)
             total = jnp.sum(across, axis=1, keepdims=True)
             rows = (1.0 - decay) * state + decay * (total / width)
-            flat = jnp.sum(jnp.where(eye, rows, 0.0), axis=0, keepdims=True)
-            rows_ref[pl.ds(slot, 1), :] = jnp.where(live, flat, 0.0)
+            rows_ref[...] = jnp.where((lane == slot) & live, rows, rows_ref[...])
             rows = jnp.broadcast_to(rows, (height, 128))
-            scale_ref[j] = lax.rsqrt(rows)
+            scale_buf[slot] = lax.rsqrt(rows)
             rows_acc[m] += fold(rows)
-            work.append((j, m, 1.0 / rows))
-        for j, m, inverse in work:
+            inverses.append((slot, m, 1.0 / rows))
+        for slot, m, inverse in inverses:
             for span in spans:
-                tile = grad_ref[j, :, span]
+                tile = grad_buf[slot, :, span]
                 weighted_acc[m, :, span] += fold(tile * tile * inverse)
-
-    @pl.when(i == pl.num_programs(0) - 1)
-    def _():
-        sums_ref[...] = jnp.zeros_like(sums_ref)
-        for m in range(mats):
-            sums_ref[m : m + 1, :] = jnp.sum(cols_acc[m], axis=0, keepdims=True)
-            sums_ref[mats + m : mats + m + 1, :] = jnp.sum(weighted_acc[m], axis=0, keepdims=True)
-            spot = lax.broadcasted_iota(jnp.int32, (1, width), 1) % cut == m
-            part = jnp.sum(rows_acc[m], axis=0, keepdims=True)[:, 0:1]
-            sums_ref[2 * mats : 2 * mats + 1, :] += jnp.where(spot, part, 0.0)
-
-
-def main_kernel(mats, row_counts, start_ref, matrix_ref, step_ref, sums_ref, state_ref, scale_ref, grad_ref, param_ref, temp_ref, cols_ref, *scratch):
-    (ids, spots, grad_buf, param_buf, scale_buf, send_buf, picked, factor, part_in, part_all, total_all) = scratch[:11]
-    (load_sem, part_sem, cross_send, cross_recv, line_send, line_recv, own_sem) = scratch[11:18]
-    recv_bufs = scratch[18:]
+        store(i).start()
+        return carry
+
+    lax.fori_loop(0, groups, work, 0)
+    sums_ref[...] = jnp.zeros_like(sums_ref)
+    for m in range(mats):
+        sums_ref[m : m + 1, :] = jnp.sum(cols_acc[m], axis=0, keepdims=True)
+        sums_ref[mats + m : mats + m + 1, :] = jnp.sum(weighted_acc[m], axis=0, keepdims=True)
+        spot = lax.broadcasted_iota(jnp.int32, (1, width), 1) % cut == m
+        part = jnp.sum(rows_acc[m], axis=0, keepdims=True)[:, 0:1]
+        sums_ref[2 * mats : 2 * mats + 1, :] += jnp.where(spot, part, 0.0)
+
+    def end_store(i, carry):
+        store(i).wait()
+        return carry
+
+    lax.fori_loop(0, groups, end_store, 0)
+
+
+def main_kernel(mats, row_counts, start_ref, matrix_ref, step_ref, state_ref, sums_in, scale_ref, grad_ref, param_ref, cols_ref, temp_ref, late_ref, *scratch):
+    (ids, spots, sums_ref, grad_buf, param_buf, scale_buf, send_buf, picked, factor, part_in, part_all, total_all) = scratch[:12]
+    (load_sem, part_sem, cross_send, cross_recv, line_send, line_recv, own_sem) = scratch[12:19]
+    recv_bufs = scratch[19:]
+    tail = late_ref.shape[0]
     parts, copies = lax.axis_size("shard"), lax.axis_size("dp")
     me, z = lax.axis_index("shard"), lax.axis_index("dp")
     row_groups, slot_count, _, width = grad_buf.shape
@@ -122,6 +141,8 @@
             device_id_type=pl.DeviceIdType.MESH,
         ).start()
 
+    sums_load = pltpu.make_async_copy(sums_in, sums_ref, part_sem.at[6])
+    sums_load.start()
     for copy in loads(0):
         copy.start()
 
@@ -130,6 +151,16 @@
         for step in range(1, size):
             peer = lax.rem(at + step, size)
             pl.semaphore_signal(barrier, inc=1, device_id={axis: peer}, device_id_type=pl.DeviceIdType.MESH)
+
+    pl.semaphore_wait(barrier, parts + copies - 2)
+    sums_load.wait()
+
+    for step in range(1, parts):
+        to = lax.rem(me + step, parts)
+        span = pl.ds(pl.multiple_of(to * cut, 128), cut)
+        send(sums_ref.at[:, span], part_in.at[me], part_sem.at[0], part_sem.at[1], "shard", to)
+    mine = pl.ds(pl.multiple_of(me * cut, 128), cut)
+    pltpu.make_async_copy(sums_ref.at[:, mine], part_in.at[me], part_sem.at[1]).start()
 
     first = start_ref[me]
 
@@ -146,14 +177,6 @@
 
     lax.fori_loop(0, slot_count, note_id, 0)
     lax.fori_loop(0, blocks, note_spot, 0)
-    pl.semaphore_wait(barrier, parts + copies - 2)
-
-    for step in range(1, parts):
-        to = lax.rem(me + step, parts)
-        span = pl.ds(pl.multiple_of(to * cut, 128), cut)
-        send(sums_ref.at[:, span], part_in.at[me], part_sem.at[0], part_sem.at[1], "shard", to)
-    mine = pl.ds(pl.multiple_of(me * cut, 128), cut)
-    pltpu.make_async_copy(sums_ref.at[:, mine], part_in.at[me], part_sem.at[1]).start()
     wait(part_in, part_sem.at[1])
     part_all[z] = jnp.sum(part_in[...], axis=0)
     for step in range(1, copies):
@@ -230,18 +253,31 @@
 
         pltpu.make_async_copy(picked.at[u], temp_ref.at[z, u], own_sem).start()
 
+    def pass_on(h, u, source, side, to, last):
+        block = temp_ref.at[source, u]
+        wait(block, line_recv.at[side, h - 1, u])
+        if h == copies - 3 and u >= units - tail:
+            @pl.when(last)
+            def _():
+                send(block, late_ref.at[u - units + tail], line_send.at[side, h], line_recv.at[side, h, u], "dp", to)
+
+            @pl.when(jnp.logical_not(last))
+            def _():
+                send(block, block, line_send.at[side, h], line_recv.at[side, h, u], "dp", to)
+        else:
+            send(block, block, line_send.at[side, h], line_recv.at[side, h, u], "dp", to)
+
     def forward(h, u):
+        if h == copies - 2 and u >= units - tail:
+            return
+
         @pl.when((z >= h) & (z < copies - 1))
         def _():
-            block = temp_ref.at[z - h, u]
-            wait(block, line_recv.at[0, h - 1, u])
-            send(block, block, line_send.at[0, h], line_recv.at[0, h, u], "dp", z + 1)
+            pass_on(h, u, z - h, 0, z + 1, z == copies - 3)
 
         @pl.when((z + h < copies) & (z > 0))
         def _():
-            block = temp_ref.at[z + h, u]
-            wait(block, line_recv.at[1, h - 1, u])
-            send(block, block, line_send.at[1, h], line_recv.at[1, h, u], "dp", z - 1)
+            pass_on(h, u, z + h, 1, z - 1, z == 2)
 
     early = min(units, 8)
     for u in range(early):
@@ -258,23 +294,34 @@
                 forward(h, i - h)
 
     for h in range(1, copies):
-        for u in range(units):
-            @pl.when((z >= h) & (z == copies - 1))
+        for u in range(units - tail if h == copies - 1 else units):
+            @pl.when(z == copies - 1)
             def _():
                 wait(temp_ref.at[z - h, u], line_recv.at[0, h - 1, u])
 
-            @pl.when((z + h < copies) & (z == 0))
+            @pl.when(z == 0)
             def _():
                 wait(temp_ref.at[z + h, u], line_recv.at[1, h - 1, u])
 
+    for t in range(tail):
+        @pl.when(z == copies - 2)
+        def _():
+            wait(late_ref.at[t], line_recv.at[0, copies - 3, units - tail + t])
+
+        @pl.when(z == 1)
+        def _():
+            wait(late_ref.at[t], line_recv.at[1, copies - 3, units - tail + t])
+
     for h in range(copies - 1):
+        sent = temp_ref.at[0, pl.ds(0, units - tail if h == copies - 2 else units)]
+
         @pl.when((z >= h) & (z < copies - 1))
         def _():
-            wait(temp_ref.at[0], line_send.at[0, h])
+            wait(sent, line_send.at[0, h])
 
         @pl.when((z + h < copies) & (z > 0))
         def _():
-            wait(temp_ref.at[0], line_send.at[1, h])
+            wait(sent, line_send.at[1, h])
 
     wait(temp_ref.at[0], own_sem)
     for u in range(units):
@@ -284,18 +331,105 @@
     wait(total_all.at[pl.ds(0, parts - 1)], part_sem.at[4])
 
 
-def place_kernel(in_ref, out_ref, buf, load_sem, store_sem):
+def late_source(copies):
+    z = lax.axis_index("dp")
+    return jnp.where(z >= copies - 2, 0, jnp.where(z <= 1, copies - 1, copies))
+
+
+def place_kernel(tail, cols_in, in_ref, late_ref, cols_out, out_ref, buf, group_load, group_store, load_sem, store_sem, late_load, late_store):
     copies, row_groups = buf.shape[0], buf.shape[1]
-    col_groups = in_ref.shape[1] // row_groups
-    where = [(d, k) for d in range(copies) for k in range(row_groups)]
-    for d, k in where:
+    units = in_ref.shape[1]
+    col_groups = units // row_groups
+    skip = late_source(copies)
+    z = lax.axis_index("dp")
+    inner = (z == 1) | (z == copies - 2)
+    cols_out[...] = cols_in[...]
+    full = (units - tail) // col_groups
+    groups = [(k, d) for k in range(full) for d in range(copies)]
+    singles = [(u, d) for u in range(full * col_groups, units) for d in range(copies)]
+
+    def load(u, d, sem):
+        k, c = u // col_groups, u % col_groups
+        return pltpu.make_async_copy(in_ref.at[d, u], buf.at[d, k, :, :, c * 128 : (c + 1) * 128], sem)
+
+    def store(u, d):
+        k, span = u // col_groups, slice(u % col_groups * 128, (u % col_groups + 1) * 128)
+        return pltpu.make_async_copy(buf.at[d, k, :, :, span], out_ref.at[:, d, k, :, span], store_sem.at[d, u])
+
+    def group_copy(k, d):
+        return pltpu.make_async_copy(buf.at[d, k], out_ref.at[:, d, k], group_store.at[d, k])
+
+    def each(u, d, work):
+        if u < units - tail:
+            work()
+        else:
+            pl.when(d != skip)(work)
+
+    for k, d in groups:
         for c in range(col_groups):
-            span = slice(c * 128, (c + 1) * 128)
-            pltpu.make_async_copy(in_ref.at[d, k * col_groups + c], buf.at[d, k, :, :, span], load_sem.at[d, k]).start()
-    for d, k in where:
-        wait(buf.at[d, k], load_sem.at[d, k])
-        pltpu.make_async_copy(buf.at[d, k], out_ref.at[:, d, k], store_sem).start()
-    wait(buf, store_sem)
+            load(k * col_groups + c, d, group_load.at[d, k]).start()
+    def load_late(u):
+        k, c = u // col_groups, u % col_groups
+        return pltpu.make_async_copy(late_ref.at[u - units + tail], buf.at[skip, k, :, :, c * 128 : (c + 1) * 128], late_load.at[u - units + tail])
+
+    def store_late(u):
+        k, span = u // col_groups, slice(u % col_groups * 128, (u % col_groups + 1) * 128)
+        return pltpu.make_async_copy(buf.at[skip, k, :, :, span], out_ref.at[:, skip, k, :, span], late_store.at[u - units + tail])
+
+    late_units = range(units - tail, units)
+    for u, d in singles:
+        each(u, d, lambda: load(u, d, load_sem.at[d, u]).start())
+
+    @pl.when(inner)
+    def _():
+        for u in late_units:
+            load_late(u).start()
+
+    for k, d in groups:
+        wait(buf.at[d, k], group_load.at[d, k])
+        group_copy(k, d).start()
+    for u, d in singles:
+        def move():
+            load(u, d, load_sem.at[d, u]).wait()
+            store(u, d).start()
+
+        each(u, d, move)
+
+    @pl.when(inner)
+    def _():
+        for u in late_units:
+            load_late(u).wait()
+            store_late(u).start()
+
+    for k, d in groups:
+        group_copy(k, d).wait()
+    for u, d in singles:
+        each(u, d, lambda: store(u, d).wait())
+
+    @pl.when(inner)
+    def _():
+        for u in late_units:
+            store_late(u).wait()
+
+
+def place_late_kernel(landed_ref, old_ref, out_ref, store_sem):
+    tail = landed_ref.shape[0]
+    copies, row_groups = out_ref.shape[1], out_ref.shape[2]
+    col_groups = out_ref.shape[4] // 128
+    z = lax.axis_index("dp")
+    skip = late_source(copies)
+
+    def store(t):
+        u = row_groups * col_groups - tail + t
+        k, span = u // col_groups, slice(u % col_groups * 128, (u % col_groups + 1) * 128)
+        return pltpu.make_async_copy(landed_ref.at[t], out_ref.at[:, skip, k, :, span], store_sem.at[t])
+
+    @pl.when((z == 0) | (z == copies - 1))
+    def _():
+        for t in range(tail):
+            store(t).start()
+        for t in range(tail):
+            store(t).wait()
 
 
 def body(parts, grad, param, row_state, col_state, block_start, block_matrix, step):
@@ -307,7 +441,9 @@
     chunks = height // CHUNK
     cut = width // parts
     copies = lax.axis_size("dp")
+    assert copies > 3
     units = chunks * (cut // 128)
+    tail = min(2, units - 1)
     row_counts = (float(D), float(D), float(FF))
 
     smem = pl.BlockSpec(memory_space=pltpu.SMEM)
@@ -315,51 +451,42 @@
     hbm = pl.BlockSpec(memory_space=pl.ANY)
     dma = pltpu.SemaphoreType.DMA
 
-    def live(i, start_ref):
-        owned = first_and_owned(start_ref, total_blocks)[1]
-        return jnp.minimum(i, (owned - 1) // group)
-
-    new_rows, scale, sums = pl.pallas_call(
+    new_rows, sums, scale = pl.pallas_call(
         functools.partial(sums_kernel, group, mats, cut),
-        grid_spec=pltpu.PrefetchScalarGridSpec(
-            num_scalar_prefetch=3,
-            grid=(steps,),
-            in_specs=[
-                pl.BlockSpec((group, height, width), lambda i, s, b, t: (live(i, s), 0, 0)),
-                pl.BlockSpec((slot_count, height), lambda i, s, b, t: (0, 0)),
-            ],
-            out_specs=[
-                pl.BlockSpec((slot_count, height), lambda i, s, b, t: (0, 0)),
-                pl.BlockSpec((group, height, 128), lambda i, s, b, t: (live(i, s), 0, 0)),
-                pl.BlockSpec((8, width), lambda i, s, b, t: (0, 0)),
-            ],
-            scratch_shapes=[
-                pltpu.VMEM((mats + 1, 8, width), jnp.float32),
-                pltpu.VMEM((mats + 1, 8, width), jnp.float32),
-                pltpu.VMEM((mats + 1, 8, 128), jnp.float32),
-            ],
-        ),
+        in_specs=[smem, smem, smem, vmem, hbm],
+        out_specs=[vmem, vmem, hbm],
         out_shape=[
-            jax.ShapeDtypeStruct((slot_count, height), jnp.float32),
+            jax.ShapeDtypeStruct((height, slot_count), jnp.float32),
+            jax.ShapeDtypeStruct((8, width), jnp.float32),
             jax.ShapeDtypeStruct((slot_count, height, 128), jnp.float32),
-            jax.ShapeDtypeStruct((8, width), jnp.float32),
+        ],
+        scratch_shapes=[
+            pltpu.VMEM((slot_count, height, width), jnp.float32),
+            pltpu.VMEM((slot_count, height, 128), jnp.float32),
+            pltpu.VMEM((mats + 1, 8, width), jnp.float32),
+            pltpu.VMEM((mats + 1, 8, width), jnp.float32),
+            pltpu.VMEM((mats + 1, 8, 128), jnp.float32),
+            dma((steps,)),
+            dma((steps,)),
         ],
         compiler_params=pltpu.CompilerParams(vmem_limit_bytes=60 * 2**20),
         cost_estimate=pl.CostEstimate(flops=grad.size * 6, bytes_accessed=grad.size * 4, transcendentals=0),
         name="sums",
-    )(block_start, block_matrix, step, grad, row_state)
-
-    temp, new_cols = pl.pallas_call(
+    )(block_start, block_matrix, step, row_state.T, grad)
+
+    new_cols, temp, late = pl.pallas_call(
         functools.partial(main_kernel, mats, row_counts),
-        in_specs=[smem, smem, smem, vmem, vmem, hbm, hbm, hbm],
-        out_specs=[hbm, vmem],
+        in_specs=[smem, smem, smem, vmem, hbm, hbm, hbm, hbm],
+        out_specs=[vmem, hbm, hbm],
         out_shape=[
+            jax.ShapeDtypeStruct((mats, width), jnp.float32),
             jax.ShapeDtypeStruct((copies, units, total_blocks, CHUNK, 128), jnp.bfloat16),
-            jax.ShapeDtypeStruct((mats, width), jnp.float32),
+            jax.ShapeDtypeStruct((tail, total_blocks, CHUNK, 128), jnp.bfloat16),
         ],
         scratch_shapes=[
             pltpu.SMEM((slot_count,), jnp.int32),
             pltpu.SMEM((total_blocks,), jnp.int32),
+            pltpu.VMEM((8, width), jnp.float32),
             pltpu.VMEM((chunks, slot_count, CHUNK, width), jnp.float32),
             pltpu.VMEM((chunks, slot_count, CHUNK, width), jnp.bfloat16),
             pltpu.VMEM((chunks, slot_count, CHUNK, 128), jnp.float32),
@@ -370,7 +497,7 @@
             pltpu.VMEM((copies, 8, cut), jnp.float32),
             pltpu.VMEM((parts, 8, cut), jnp.float32),
             dma((3, chunks)),
-            dma((6,)),
+            dma((7,)),
             dma((units,)),
             dma((units,)),
             dma((2, copies - 1)),
@@ -383,24 +510,44 @@
         ),
         cost_estimate=pl.CostEstimate(flops=grad.size * 6, bytes_accessed=grad.size * 8, transcendentals=0),
         name="main",
-    )(block_start, block_matrix, step, sums, col_state, scale, grad, param)
-
-    placed = pl.pallas_call(
-        place_kernel,
-        in_specs=[hbm],
-        out_specs=hbm,
-        out_shape=jax.ShapeDtypeStruct((total_blocks, copies, chunks, CHUNK, cut), jnp.bfloat16),
+    )(block_start, block_matrix, step, col_state, sums, scale, grad, param)
+
+    landed = lax.ppermute(late, "dp", [(copies - 2, copies - 1), (1, 0)])
+    size = total_blocks * copies * height * cut
+    placed_shape = jax.ShapeDtypeStruct((total_blocks, copies, chunks, CHUNK, cut), jnp.bfloat16)
+    new_cols, placed = pl.pallas_call(
+        functools.partial(place_kernel, tail),
+        in_specs=[vmem, hbm, hbm],
+        out_specs=[vmem, hbm],
+        out_shape=[jax.ShapeDtypeStruct((mats, width), jnp.float32), placed_shape],
         scratch_shapes=[
             pltpu.VMEM((copies, chunks, total_blocks, CHUNK, cut), jnp.bfloat16),
             dma((copies, chunks)),
-            dma(()),
+            dma((copies, chunks)),
+            dma((copies, units)),
+            dma((copies, units)),
+            dma((tail,)),
+            dma((tail,)),
         ],
         compiler_params=pltpu.CompilerParams(vmem_limit_bytes=60 * 2**20),
-        cost_estimate=pl.CostEstimate(flops=0, bytes_accessed=2 * total_blocks * copies * height * cut * 2, transcendentals=0),
+        cost_estimate=pl.CostEstimate(flops=size * 10, bytes_accessed=4 * size, transcendentals=0),
         name="place",
-    )(temp)
+    )(new_cols, temp, late)
+    placed = pl.pallas_call(
+        place_late_kernel,
+        in_specs=[hbm, hbm],
+        out_specs=hbm,
+        out_shape=placed_shape,
+        input_output_aliases={1: 0},
+        scratch_shapes=[
+            dma((tail,)),
+        ],
+        compiler_params=pltpu.CompilerParams(vmem_limit_bytes=4 * 2**20),
+        cost_estimate=pl.CostEstimate(flops=size, bytes_accessed=size, transcendentals=0),
+        name="place_late",
+    )(landed, placed)
     new_params = placed.reshape(total_blocks * copies * height, cut)
-    return new_params, new_rows, new_cols
+    return new_params, new_rows.T, new_cols
 
 
 def solution(mesh):

time: 364 us -> 350 us (0.962)
  Pallas kernels: 358 us -> 346 us
    pallas_call x1, Pallas kernels: 333 us -> 321 us  [body(): pl.pallas_call(functools.partial(main_kernel, mats, row_counts), in_specs...]
    pallas_call x2 -> x3, Pallas kernels: 24.2 us -> 25.6 us  [the longest x1 15.7 us: body(): pl.pallas_call(functools.partial(place_kernel, tail), in_specs=[vmem, hbm...]
  transfers between devices with their start and end apart: 0 -> 1, of which waited for: 0 -> 1; matrix products, arithmetic and copies ran while one was open for 0% -> 0% of each run, Pallas kernels for 0% -> 4%
where the time goes in v3:
time: 350 us
  Pallas kernels  346 us (99%)
    pallas_call x1, Pallas kernels, body(): pl.pallas_call(functools.partial(main_kernel, mats, row_counts), in_specs...  321 us
    pallas_call x1, Pallas kernels, body(): pl.pallas_call(functools.partial(place_kernel, tail), in_specs=[vmem, hbm...  15.7 us
    pallas_call x1, Pallas kernels, body(): pl.pallas_call(functools.partial(sums_kernel, group, mats, cut), in_specs...  9.11 us
  transfers between devices with their start and end apart: 1, of which 1 were waited for; matrix products, arithmetic and copies ran while one was open for 0% of the time, Pallas kernels for 4%

profile of v3, /device:TPU:0, one launch (start us, length us, event | category | flops | bytes accessed | tf_op | source)
XLA Modules:
  0.0 350.2 jit_solution(16648999393739394720)
XLA Ops:
  1.3 9.1 %sums.1 = (f32[32,36]{1,0:T(8,128)}, f32[8,4096]{1,0:T(8,128)}, f32[36,32,128]{2,1,0:T(8,128)}) custom-call(s32[8]{0:T(128)} %start_ref.3, s32[144]{0:T(256)} %matrix_ref.3, s32[1]{0:T(128)S(6)} %copy.12.step_ref, f32[32,36]{1,0:T(8,128)} %bitcast.4, f32[36,32,4096]{2,1,0:T(8,128)} %grad_ref.3), custom_call_target="tpu_custom_call" | custom-call | flops 28311552 | bytes 18874368 | tf_op jit(solution)/shard_map/sums/pallas_call | solution.py:454
  10.4 320.7 %main.1 = (f32[3,4096]{1,0:T(4,128)}, bf16[4,16,144,8,128]{4,3,2,1,0:T(8,128)(2,1)}, bf16[2,144,8,128]{3,2,1,0:T(8,128)(2,1)}) custom-call(s32[8]{0:T(128)} %start_ref.3, s32[144]{0:T(256)} %matrix_ref.3, s32[1]{0:T(128)S(6)} %copy.12.step_ref, f32[3,4096]{1,0:T(4,128)} %state_ref.1, f32[8,4096]{1,0:T(8,128)} %get-tuple-element.11.sums_in, ...), custom_call_target="tpu_custom_call" | custom-call | flops 28311552 | bytes 37748736 | tf_op jit(solution)/shard_map/main/pallas_call | solution.py:477
  331.1 1.3 collective-permute-start
  332.4 15.7 %place.1 = (f32[3,4096]{1,0:T(4,128)}, bf16[144,4,4,8,512]{4,3,2,1,0:T(8,128)(2,1)}) custom-call(f32[3,4096]{1,0:T(4,128)} %get-tuple-element.14.cols_in, bf16[4,16,144,8,128]{4,3,2,1,0:T(8,128)(2,1)} %get-tuple-element.15.in_ref, bf16[2,144,8,128]{3,2,1,0:T(8,128)(2,1)} %get-tuple-element.13.late_ref), custom_call_target="tpu_custom_call" | custom-call | flops 94371840 | bytes 37748736 | tf_op jit(solution)/shard_map/place/pallas_call | solution.py:518
  348.1 1.3 collective-permute-done.landed_ref
  349.3 0.8 place_late.1
Async XLA Ops:
  331.1 18.3 %collective-permute-start = (bf16[2,144,8,128]{3,2,1,0:T(8,128)(2,1)}, bf16[2,144,8,128]{3,2,1,0:T(8,128)(2,1)S(1)}, u32[]{:S(2)}, u32[]{:S(2)}) collective-permute-start(bf16[2,144,8,128]{3,2,1,0:T(8,128)(2,1)} %get-tuple-element.13.late_ref), channel_id=1, source_target_pairs={{2,3},{1,0},{6,7},{5,4},{10,11},{9,8},{14,15},{13,12},{18,19},{17,... | collective-permute-start | bytes 1769480 | tf_op jit(solution)/shard_map/ppermute | solution.py:515

commit v4 on v3

--- a/solution.py
+++ b/solution.py
@@ -33,88 +33,10 @@
     return jnp.exp(-0.8 * jnp.log(jnp.full(shape, step_ref[0], jnp.int32).astype(jnp.float32)))
 
 
-def sums_kernel(group, mats, cut, start_ref, matrix_ref, step_ref, state_ref, grad_ref, rows_ref, sums_ref, scale_ref, grad_buf, scale_buf, cols_acc, weighted_acc, rows_acc, load_sem, store_sem):
-    blocks = matrix_ref.shape[0]
-    first, owned = first_and_owned(start_ref, blocks)
-    groups = (owned + group - 1) // group
-    height, width = grad_ref.shape[1], grad_ref.shape[2]
-    spans = [slice(n, n + 128) for n in range(0, width, 128)]
-
-    def load(i):
-        slots = pl.ds(i * group, group)
-        return pltpu.make_async_copy(grad_ref.at[slots], grad_buf.at[slots], load_sem.at[i])
-
-    def store(i):
-        slots = pl.ds(i * group, group)
-        return pltpu.make_async_copy(scale_buf.at[slots], scale_ref.at[slots], store_sem.at[i])
-
-    def start_load(i, carry):
-        load(i).start()
-        return carry
-
-    lax.fori_loop(0, groups, start_load, 0)
-
-    def fold(tile):
-        parts = [tile[n : n + 8] for n in range(0, height, 8)]
-        while len(parts) > 1:
-            parts = [a + b for a, b in zip(parts[::2], parts[1::2])] + parts[len(parts) & ~1 :]
-        return parts[0]
-
-    rows_ref[...] = jnp.zeros_like(rows_ref)
-    cols_acc[...] = jnp.zeros_like(cols_acc)
-    weighted_acc[...] = jnp.zeros_like(weighted_acc)
-    rows_acc[...] = jnp.zeros_like(rows_acc)
-    decay = decay_of(step_ref, (height, 1))
-    lane = lax.broadcasted_iota(jnp.int32, rows_ref.shape, 1)
-
-    def work(i, carry):
-        load(i).wait()
-        inverses = []
-        for j in range(group):
-            slot = i * group + j
-            live = slot < owned
-            m = jnp.where(live, matrix_ref[jnp.minimum(first + slot, blocks - 1)], mats)
-            across = jnp.zeros((height, 128), jnp.float32)
-            for span in spans:
-                tile = grad_buf[slot, :, span]
-                tile = tile * tile
-                across += tile
-                cols_acc[m, :, span] += fold(tile)
-            state = jnp.sum(jnp.where(lane == slot, state_ref[...], 0.0), axis=1, keepdims=True)
-            total = jnp.sum(across, axis=1, keepdims=True)
-            rows = (1.0 - decay) * state + decay * (total / width)
-            rows_ref[...] = jnp.where((lane == slot) & live, rows, rows_ref[...])
-            rows = jnp.broadcast_to(rows, (height, 128))
-            scale_buf[slot] = lax.rsqrt(rows)
-            rows_acc[m] += fold(rows)
-            inverses.append((slot, m, 1.0 / rows))
-        for slot, m, inverse in inverses:
-            for span in spans:
-                tile = grad_buf[slot, :, span]
-                weighted_acc[m, :, span] += fold(tile * tile * inverse)
-        store(i).start()
-        return carry
-
-    lax.fori_loop(0, groups, work, 0)
-    sums_ref[...] = jnp.zeros_like(sums_ref)
-    for m in range(mats):
-        sums_ref[m : m + 1, :] = jnp.sum(cols_acc[m], axis=0, keepdims=True)
-        sums_ref[mats + m : mats + m + 1, :] = jnp.sum(weighted_acc[m], axis=0, keepdims=True)
-        spot = lax.broadcasted_iota(jnp.int32, (1, width), 1) % cut == m
-        part = jnp.sum(rows_acc[m], axis=0, keepdims=True)[:, 0:1]
-        sums_ref[2 * mats : 2 * mats + 1, :] += jnp.where(spot, part, 0.0)
-
-    def end_store(i, carry):
-        store(i).wait()
-        return carry
-
-    lax.fori_loop(0, groups, end_store, 0)
-
-
-def main_kernel(mats, row_counts, start_ref, matrix_ref, step_ref, state_ref, sums_in, scale_ref, grad_ref, param_ref, cols_ref, temp_ref, late_ref, *scratch):
+def main_kernel(mats, group, row_counts, start_ref, matrix_ref, step_ref, state_ref, row_state_ref, grad_ref, param_ref, cols_ref, rows_ref, temp_ref, late_ref, *scratch):
     (ids, spots, sums_ref, grad_buf, param_buf, scale_buf, send_buf, picked, factor, part_in, part_all, total_all) = scratch[:12]
-    (load_sem, part_sem, cross_send, cross_recv, line_send, line_recv, own_sem) = scratch[12:19]
-    recv_bufs = scratch[19:]
+    (cols_acc, weighted_acc, rows_acc, grad_sem, param_sem, part_sem, cross_send, cross_recv, line_send, line_recv, own_sem) = scratch[12:23]
+    recv_bufs = scratch[23:]
     tail = late_ref.shape[0]
     parts, copies = lax.axis_size("shard"), lax.axis_size("dp")
     me, z = lax.axis_index("shard"), lax.axis_index("dp")
@@ -123,13 +45,9 @@
     cut = width // parts
     col_groups = units // row_groups
     blocks = picked.shape[1]
-    def loads(k):
+    def param_load(k):
         rows = pl.ds(k * CHUNK, CHUNK)
-        return (
-            pltpu.make_async_copy(grad_ref.at[:, rows, :], grad_buf.at[k], load_sem.at[0, k]),
-            pltpu.make_async_copy(param_ref.at[:, rows, :], param_buf.at[k], load_sem.at[1, k]),
-            pltpu.make_async_copy(scale_ref.at[:, rows, :], scale_buf.at[k], load_sem.at[2, k]),
-        )
+        return pltpu.make_async_copy(param_ref.at[:, rows, :], param_buf.at[k], param_sem.at[k])
 
     def send(src, dst, send_sem, recv_sem, axis, to):
         pltpu.make_async_remote_copy(
@@ -141,10 +59,11 @@
             device_id_type=pl.DeviceIdType.MESH,
         ).start()
 
-    sums_load = pltpu.make_async_copy(sums_in, sums_ref, part_sem.at[6])
-    sums_load.start()
-    for copy in loads(0):
-        copy.start()
+    for i in range(slot_count // group):
+        slots = pl.ds(i * group, group)
+        for k in range(row_groups):
+            rows = pl.ds(k * CHUNK, CHUNK)
+            pltpu.make_async_copy(grad_ref.at[slots, rows, :], grad_buf.at[k, slots], grad_sem.at[i]).start()
 
     barrier = pltpu.get_barrier_semaphore()
     for axis, at, size in (("shard", me, parts), ("dp", z, copies)):
@@ -152,8 +71,73 @@
             peer = lax.rem(at + step, size)
             pl.semaphore_signal(barrier, inc=1, device_id={axis: peer}, device_id_type=pl.DeviceIdType.MESH)
 
+    first, owned = first_and_owned(start_ref, blocks)
+
+    def note_id(j, carry):
+        ids[j] = jnp.where(j < owned, matrix_ref[jnp.minimum(first + j, blocks - 1)], mats)
+        return carry
+
+    lax.fori_loop(0, slot_count, note_id, 0)
+
+    decay = decay_of(step_ref, (1, 1))
+    cols_acc[...] = jnp.zeros_like(cols_acc)
+    weighted_acc[...] = jnp.zeros_like(weighted_acc)
+    rows_acc[...] = jnp.zeros_like(rows_acc)
+    rows_ref[...] = jnp.zeros_like(rows_ref)
+    lane = lax.broadcasted_iota(jnp.int32, (CHUNK, slot_count), 1)
+    spans = [slice(n, n + 128) for n in range(0, width, 128)]
+
+    def add_to(acc, m, span, value):
+        for n in range(mats):
+            acc[n, :, span] += jnp.where(m == n, value, 0.0)
+
+    def total_of(values):
+        while len(values) > 1:
+            values = [a + b for a, b in zip(values[::2], values[1::2])] + values[len(values) & ~1 :]
+        return values[0]
+
+    def work(i, carry):
+        wait(grad_buf.at[:, pl.ds(i * group, group)], grad_sem.at[i])
+        inverses = []
+        for j in range(group):
+            slot = i * group + j
+            m = ids[slot]
+            across = [jnp.zeros((CHUNK, 128), jnp.float32)] * row_groups
+            for span in spans:
+                tiles = [grad_buf[k, slot, :, span] for k in range(row_groups)]
+                tiles = [tile * tile for tile in tiles]
+                across = [a + b for a, b in zip(across, tiles)]
+                add_to(cols_acc, m, span, total_of(tiles))
+            inverse = []
+            for k in range(row_groups):
+                at = slice(k * CHUNK, (k + 1) * CHUNK)
+                here = lane == slot
+                state = jnp.sum(jnp.where(here, row_state_ref[at, :], 0.0), axis=1, keepdims=True)
+                rows = (1.0 - decay) * state + decay * (jnp.sum(across[k], axis=1, keepdims=True) / width)
+                rows_ref[at, :] = jnp.where(here & (m < mats), rows, rows_ref[at, :])
+                rows = jnp.broadcast_to(rows, (CHUNK, 128))
+                scale_buf[k, slot] = lax.rsqrt(rows)
+                add_to(rows_acc, m, slice(0, 128), rows)
+                inverse.append(1.0 / rows)
+            inverses.append((slot, m, inverse))
+        for slot, m, inverse in inverses:
+            for span in spans:
+                tiles = [grad_buf[k, slot, :, span] for k in range(row_groups)]
+                add_to(weighted_acc, m, span, total_of([tile * tile * inverse[k] for k, tile in enumerate(tiles)]))
+        return carry
+
+    lax.fori_loop(0, slot_count // group, work, 0)
+    for k in range(row_groups):
+        param_load(k).start()
+    for m in range(mats):
+        sums_ref[m : m + 1, :] = jnp.sum(cols_acc[m], axis=0, keepdims=True)
+        sums_ref[mats + m : mats + m + 1, :] = jnp.sum(weighted_acc[m], axis=0, keepdims=True)
+    spot = lax.broadcasted_iota(jnp.int32, (1, width), 1) % cut
+    rest = jnp.zeros((1, width), jnp.float32)
+    for m in range(mats):
+        rest = jnp.where(spot == m, jnp.sum(rows_acc[m], axis=0, keepdims=True)[:, 0:1], rest)
+    sums_ref[2 * mats :, :] = jnp.broadcast_to(rest, (8 - 2 * mats, width))
     pl.semaphore_wait(barrier, parts + copies - 2)
-    sums_load.wait()
 
     for step in range(1, parts):
         to = lax.rem(me + step, parts)
@@ -162,12 +146,6 @@
     mine = pl.ds(pl.multiple_of(me * cut, 128), cut)
     pltpu.make_async_copy(sums_ref.at[:, mine], part_in.at[me], part_sem.at[1]).start()
 
-    first = start_ref[me]
-
-    def note_id(j, carry):
-        ids[j] = matrix_ref[jnp.minimum(first + j, blocks - 1)]
-        return carry
-
     def note_spot(b, carry):
         shift = jnp.int32(0)
         for s in range(1, parts):
@@ -175,7 +153,6 @@
         spots[b] = jnp.minimum(b + shift, parts * slot_count - 1)
         return carry
 
-    lax.fori_loop(0, slot_count, note_id, 0)
     lax.fori_loop(0, blocks, note_spot, 0)
     wait(part_in, part_sem.at[1])
     part_all[z] = jnp.sum(part_in[...], axis=0)
@@ -183,43 +160,44 @@
         to = lax.rem(z + step, copies)
         send(part_all.at[z], part_all.at[z], part_sem.at[2], part_sem.at[3], "dp", to)
     wait(part_all.at[pl.ds(0, copies - 1)], part_sem.at[3])
-    total_all[me] = jnp.sum(part_all[...], axis=0)
+    total = jnp.sum(part_all[...], axis=0)
+    lanes = lax.broadcasted_iota(jnp.int32, (1, cut), 1)
+    partial = jnp.zeros((1, cut), jnp.float32)
+    for m in range(mats):
+        cols = (1.0 - decay) * state_ref[m : m + 1, mine] + decay * (total[m : m + 1] / row_counts[m])
+        total_all[me, m : m + 1, :] = cols
+        partial = jnp.where(lanes == m, jnp.sum(total[mats + m : mats + m + 1] / cols, axis=1, keepdims=True), partial)
+    total_all[me, mats : mats + 1, :] = partial
     for step in range(1, parts):
         to = lax.rem(me + step, parts)
         send(total_all.at[me], total_all.at[me], part_sem.at[4], part_sem.at[5], "shard", to)
-    for k in range(1, row_groups):
-        for copy in loads(k):
-            copy.start()
     wait(total_all.at[pl.ds(0, parts - 1)], part_sem.at[5])
 
-    decay = decay_of(step_ref, (1, 1))
     step = jnp.full((1, 1), step_ref[0], jnp.int32).astype(jnp.float32)
     rate = 1.0 / jnp.sqrt(jnp.maximum(step, 10000.0))
+    squares = total_all[0, mats : mats + 1, :]
+    for s in range(1, parts):
+        squares += total_all[s, mats : mats + 1, :]
     for m in range(mats):
         count = row_counts[m]
-        square = jnp.zeros((1, 1), jnp.float32)
-        for s in range(parts):
-            span = slice(s * cut, (s + 1) * cut)
-            cols = (1.0 - decay) * state_ref[m : m + 1, span] + decay * (total_all[s, m : m + 1, :] / count)
-            cols_ref[m : m + 1, span] = cols
-            square += jnp.sum(total_all[s, mats + m : mats + m + 1, :] / cols, axis=1, keepdims=True)
-        average = total_all[0, 2 * mats : 2 * mats + 1, m : m + 1] / count
-        clip = jnp.maximum(1.0, jnp.sqrt(average * square / (count * width)))
+        average = total[2 * mats : 2 * mats + 1, m : m + 1] / count
+        clip = jnp.maximum(1.0, jnp.sqrt(average * squares[:, m : m + 1] / (count * width)))
         gain = jnp.sqrt(average) * rate / clip
         for s in range(parts):
             span = slice(s * cut, (s + 1) * cut)
-            factor[m, :, span] = jnp.broadcast_to(lax.rsqrt(cols_ref[m : m + 1, span]) * gain, (CHUNK, cut))
+            cols = total_all[s, m : m + 1, :]
+            cols_ref[m : m + 1, span] = cols
+            factor[m, :, span] = jnp.broadcast_to(lax.rsqrt(cols) * gain, (CHUNK, cut))
 
     unroll = largest(4, slot_count)
 
     def update(u):
         k, c = u // col_groups, u % col_groups
         if c == 0:
-            for copy in loads(k):
-                copy.wait()
+            param_load(k).wait()
 
         def slot(j, carry):
-            m = ids[j]
+            m = jnp.minimum(ids[j], mats - 1)
             scale = scale_buf[k, j]
             for s in range(parts):
                 span = slice(s * cut + c * 128, s * cut + (c + 1) * 128)
@@ -229,9 +207,14 @@
 
         lax.fori_loop(0, slot_count, slot, 0, unroll=unroll)
         spot = pl.ds(me * slot_count, slot_count)
-        for step in range(1, parts):
-            to = lax.rem(me + step, parts)
-            send(send_buf.at[u, to], recv_bufs[u].at[spot], cross_send.at[u], cross_recv.at[u], "shard", to)
+        for core in (1, 0):
+            for step in range(parts // 2):
+                to = lax.rem(me // 2 + step, parts // 2) * 2 + core
+
+                @pl.when(to != me)
+                def _():
+                    send(send_buf.at[u, to], recv_bufs[u].at[spot], cross_send.at[u], cross_recv.at[u], "shard", to)
+
         pltpu.make_async_copy(send_buf.at[u, me], recv_bufs[u].at[spot], cross_recv.at[u]).start()
 
     def own(u):
@@ -336,7 +319,7 @@
     return jnp.where(z >= copies - 2, 0, jnp.where(z <= 1, copies - 1, copies))
 
 
-def place_kernel(tail, cols_in, in_ref, late_ref, cols_out, out_ref, buf, group_load, group_store, load_sem, store_sem, late_load, late_store):
+def place_kernel(tail, cols_in, rows_in, in_ref, late_ref, cols_out, rows_out, out_ref, buf, group_load, group_store, load_sem, store_sem, late_load, late_store):
     copies, row_groups = buf.shape[0], buf.shape[1]
     units = in_ref.shape[1]
     col_groups = units // row_groups
@@ -344,6 +327,7 @@
     z = lax.axis_index("dp")
     inner = (z == 1) | (z == copies - 2)
     cols_out[...] = cols_in[...]
+    rows_out[...] = rows_in[...]
     full = (units - tail) // col_groups
     groups = [(k, d) for k in range(full) for d in range(copies)]
     singles = [(u, d) for u in range(full * col_groups, units) for d in range(copies)]
@@ -451,35 +435,13 @@
     hbm = pl.BlockSpec(memory_space=pl.ANY)
     dma = pltpu.SemaphoreType.DMA
 
-    new_rows, sums, scale = pl.pallas_call(
-        functools.partial(sums_kernel, group, mats, cut),
-        in_specs=[smem, smem, smem, vmem, hbm],
-        out_specs=[vmem, vmem, hbm],
-        out_shape=[
-            jax.ShapeDtypeStruct((height, slot_count), jnp.float32),
-            jax.ShapeDtypeStruct((8, width), jnp.float32),
-            jax.ShapeDtypeStruct((slot_count, height, 128), jnp.float32),
-        ],
-        scratch_shapes=[
-            pltpu.VMEM((slot_count, height, width), jnp.float32),
-            pltpu.VMEM((slot_count, height, 128), jnp.float32),
-            pltpu.VMEM((mats + 1, 8, width), jnp.float32),
-            pltpu.VMEM((mats + 1, 8, width), jnp.float32),
-            pltpu.VMEM((mats + 1, 8, 128), jnp.float32),
-            dma((steps,)),
-            dma((steps,)),
-        ],
-        compiler_params=pltpu.CompilerParams(vmem_limit_bytes=60 * 2**20),
-        cost_estimate=pl.CostEstimate(flops=grad.size * 6, bytes_accessed=grad.size * 4, transcendentals=0),
-        name="sums",
-    )(block_start, block_matrix, step, row_state.T, grad)
-
-    new_cols, temp, late = pl.pallas_call(
-        functools.partial(main_kernel, mats, row_counts),
-        in_specs=[smem, smem, smem, vmem, hbm, hbm, hbm, hbm],
-        out_specs=[vmem, hbm, hbm],
+    new_cols, new_rows, temp, late = pl.pallas_call(
+        functools.partial(main_kernel, mats, group, row_counts),
+        in_specs=[smem, smem, smem, vmem, vmem, hbm, hbm],
+        out_specs=[vmem, vmem, hbm, hbm],
         out_shape=[
             jax.ShapeDtypeStruct((mats, width), jnp.float32),
+            jax.ShapeDtypeStruct((height, slot_count), jnp.float32),
             jax.ShapeDtypeStruct((copies, units, total_blocks, CHUNK, 128), jnp.bfloat16),
             jax.ShapeDtypeStruct((tail, total_blocks, CHUNK, 128), jnp.bfloat16),
         ],
@@ -495,9 +457,13 @@
             pltpu.VMEM((mats, CHUNK, width), jnp.float32),
             pltpu.VMEM((parts, 8, cut), jnp.float32),
             pltpu.VMEM((copies, 8, cut), jnp.float32),
-            pltpu.VMEM((parts, 8, cut), jnp.float32),
-            dma((3, chunks)),
-            dma((7,)),
+            pltpu.VMEM((parts, mats + 1, cut), jnp.float32),
+            pltpu.VMEM((mats, CHUNK, width), jnp.float32),
+            pltpu.VMEM((mats, CHUNK, width), jnp.float32),
+            pltpu.VMEM((mats, CHUNK, 128), jnp.float32),
+            dma((steps,)),
+            dma((chunks,)),
+            dma((6,)),
             dma((units,)),
             dma((units,)),
             dma((2, copies - 1)),
@@ -510,16 +476,20 @@
         ),
         cost_estimate=pl.CostEstimate(flops=grad.size * 6, bytes_accessed=grad.size * 8, transcendentals=0),
         name="main",
-    )(block_start, block_matrix, step, col_state, sums, scale, grad, param)
+    )(block_start, block_matrix, step, col_state, row_state.T, grad, param)
 
     landed = lax.ppermute(late, "dp", [(copies - 2, copies - 1), (1, 0)])
     size = total_blocks * copies * height * cut
     placed_shape = jax.ShapeDtypeStruct((total_blocks, copies, chunks, CHUNK, cut), jnp.bfloat16)
-    new_cols, placed = pl.pallas_call(
+    new_cols, new_rows, placed = pl.pallas_call(
         functools.partial(place_kernel, tail),
-        in_specs=[vmem, hbm, hbm],
-        out_specs=[vmem, hbm],
-        out_shape=[jax.ShapeDtypeStruct((mats, width), jnp.float32), placed_shape],
+        in_specs=[vmem, vmem, hbm, hbm],
+        out_specs=[vmem, vmem, hbm],
+        out_shape=[
+            jax.ShapeDtypeStruct((mats, width), jnp.float32),
+            jax.ShapeDtypeStruct((height, slot_count), jnp.float32),
+            placed_shape,
+        ],
         scratch_shapes=[
             pltpu.VMEM((copies, chunks, total_blocks, CHUNK, cut), jnp.bfloat16),
             dma((copies, chunks)),
@@ -532,7 +502,7 @@
         compiler_params=pltpu.CompilerParams(vmem_limit_bytes=60 * 2**20),
         cost_estimate=pl.CostEstimate(flops=size * 10, bytes_accessed=4 * size, transcendentals=0),
         name="place",
-    )(new_cols, temp, late)
+    )(new_cols, new_rows, temp, late)
     placed = pl.pallas_call(
         place_late_kernel,
         in_specs=[hbm, hbm],

time: 350 us -> 344 us (0.983)
  Pallas kernels: 346 us -> 341 us
    pallas_call x3 -> x2, Pallas kernels: 345 us -> 341 us  [the longest x1 325 us: body(): pl.pallas_call(functools.partial(main_kernel, mats, group, row_counts), i...]
  transfers between devices with their start and end apart: 1 -> 1, of which waited for: 1 -> 0; matrix products, arithmetic and copies ran while one was open for 0% -> 0% of each run, Pallas kernels for 4% -> 5%
where the time goes in v4:
time: 344 us
  Pallas kernels  341 us (99%)
    pallas_call x1, Pallas kernels, body(): pl.pallas_call(functools.partial(main_kernel, mats, group, row_counts), i...  325 us
    pallas_call x1, Pallas kernels, body(): pl.pallas_call(functools.partial(place_kernel, tail), in_specs=[vmem, vme...  15.7 us
  transfers between devices with their start and end apart: 1, of which 0 were waited for; matrix products, arithmetic and copies ran while one was open for 0% of the time, Pallas kernels for 5%

profile of v4, /device:TPU:0, one launch (start us, length us, event | category | flops | bytes accessed | tf_op | source)
XLA Modules:
  0.0 344.1 jit_solution(291025310678601542)
XLA Ops:
  1.3 324.9 %main.1 = (f32[3,4096]{1,0:T(4,128)}, f32[32,36]{1,0:T(8,128)}, bf16[4,16,144,8,128]{4,3,2,1,0:T(8,128)(2,1)}, bf16[2,144,8,128]{3,2,1,0:T(8,128)(2,1)}) custom-call(s32[8]{0:T(128)} %start_ref.1, s32[144]{0:T(256)} %matrix_ref.1, s32[1]{0:T(128)S(6)} %copy.12.step_ref, f32[3,4096]{1,0:T(4,128)} %state_ref.1, f32[32,36]{1,0:T(8,128)} %bitcast.4, ...), custom_call_target="tpu_custom_call" | custom-call | flops 28311552 | bytes 37748736 | tf_op jit(solution)/shard_map/main/pallas_call | solution.py:438
  326.2 1.3 collective-permute-start
  327.5 15.7 %place.1 = (f32[3,4096]{1,0:T(4,128)}, f32[32,36]{1,0:T(8,128)}, bf16[144,4,4,8,512]{4,3,2,1,0:T(8,128)(2,1)}) custom-call(f32[3,4096]{1,0:T(4,128)} %get-tuple-element.11.cols_in, f32[32,36]{1,0:T(8,128)} %get-tuple-element.12.rows_in, bf16[4,16,144,8,128]{4,3,2,1,0:T(8,128)(2,1)} %get-tuple-element.13.in_ref, ...), custom_call_target="tpu_custom_call" | custom-call | flops 94371840 | bytes 37748736 | tf_op jit(solution)/shard_map/place/pallas_call | solution.py:484
  343.2 0.0 collective-permute-done.landed_ref
  343.2 0.8 place_late.1
Async XLA Ops:
  326.2 17.0 %collective-permute-start = (bf16[2,144,8,128]{3,2,1,0:T(8,128)(2,1)}, bf16[2,144,8,128]{3,2,1,0:T(8,128)(2,1)S(1)}, u32[]{:S(2)}, u32[]{:S(2)}) collective-permute-start(bf16[2,144,8,128]{3,2,1,0:T(8,128)(2,1)} %get-tuple-element.10.late_ref), channel_id=1, source_target_pairs={{2,3},{1,0},{6,7},{5,4},{10,11},{9,8},{14,15},{13,12},{18,19},{17,... | collective-permute-start | bytes 1769480 | tf_op jit(solution)/shard_map/ppermute | solution.py:481

commit v5 on v4

--- a/solution.py
+++ b/solution.py
@@ -33,10 +33,15 @@
     return jnp.exp(-0.8 * jnp.log(jnp.full(shape, step_ref[0], jnp.int32).astype(jnp.float32)))
 
 
-def main_kernel(mats, group, row_counts, start_ref, matrix_ref, step_ref, state_ref, row_state_ref, grad_ref, param_ref, cols_ref, rows_ref, temp_ref, late_ref, *scratch):
+def main_kernel(mats, group, row_counts, start_ref, matrix_ref, step_ref, state_ref, row_state_ref, grad_ref, param_ref, cols_out, rows_out, temp_ref, late_ref, *scratch):
     (ids, spots, sums_ref, grad_buf, param_buf, scale_buf, send_buf, picked, factor, part_in, part_all, total_all) = scratch[:12]
     (cols_acc, weighted_acc, rows_acc, grad_sem, param_sem, part_sem, cross_send, cross_recv, line_send, line_recv, own_sem) = scratch[12:23]
-    recv_bufs = scratch[23:]
+    (cols_ref, rows_ref, small_sem) = scratch[23:26]
+    recv_bufs = scratch[26:]
+    small_stores = [
+        pltpu.make_async_copy(rows_ref, rows_out, small_sem.at[2]),
+        pltpu.make_async_copy(cols_ref, cols_out, small_sem.at[3]),
+    ]
     tail = late_ref.shape[0]
     parts, copies = lax.axis_size("shard"), lax.axis_size("dp")
     me, z = lax.axis_index("shard"), lax.axis_index("dp")
@@ -87,9 +92,9 @@
     lane = lax.broadcasted_iota(jnp.int32, (CHUNK, slot_count), 1)
     spans = [slice(n, n + 128) for n in range(0, width, 128)]
 
-    def add_to(acc, m, span, value):
+    def add_to(acc, ms, span, values):
         for n in range(mats):
-            acc[n, :, span] += jnp.where(m == n, value, 0.0)
+            acc[n, :, span] += total_of([jnp.where(m == n, value, 0.0) for m, value in zip(ms, values)])
 
     def total_of(values):
         while len(values) > 1:
@@ -98,32 +103,37 @@
 
     def work(i, carry):
         wait(grad_buf.at[:, pl.ds(i * group, group)], grad_sem.at[i])
-        inverses = []
-        for j in range(group):
-            slot = i * group + j
-            m = ids[slot]
-            across = [jnp.zeros((CHUNK, 128), jnp.float32)] * row_groups
-            for span in spans:
+        slots = [i * group + j for j in range(group)]
+        ms = [ids[slot] for slot in slots]
+        across = [[jnp.zeros((CHUNK, 128), jnp.float32)] * row_groups for _ in slots]
+        for span in spans:
+            totals = []
+            for j, slot in enumerate(slots):
                 tiles = [grad_buf[k, slot, :, span] for k in range(row_groups)]
                 tiles = [tile * tile for tile in tiles]
-                across = [a + b for a, b in zip(across, tiles)]
-                add_to(cols_acc, m, span, total_of(tiles))
-            inverse = []
-            for k in range(row_groups):
-                at = slice(k * CHUNK, (k + 1) * CHUNK)
+                across[j] = [a + b for a, b in zip(across[j], tiles)]
+                totals.append(total_of(tiles))
+            add_to(cols_acc, ms, span, totals)
+        inverses = []
+        for k in range(row_groups):
+            at = slice(k * CHUNK, (k + 1) * CHUNK)
+            found = []
+            for j, slot in enumerate(slots):
                 here = lane == slot
                 state = jnp.sum(jnp.where(here, row_state_ref[at, :], 0.0), axis=1, keepdims=True)
-                rows = (1.0 - decay) * state + decay * (jnp.sum(across[k], axis=1, keepdims=True) / width)
-                rows_ref[at, :] = jnp.where(here & (m < mats), rows, rows_ref[at, :])
+                rows = (1.0 - decay) * state + decay * (jnp.sum(across[j][k], axis=1, keepdims=True) / width)
+                rows_ref[at, :] = jnp.where(here & (ms[j] < mats), rows, rows_ref[at, :])
                 rows = jnp.broadcast_to(rows, (CHUNK, 128))
                 scale_buf[k, slot] = lax.rsqrt(rows)
-                add_to(rows_acc, m, slice(0, 128), rows)
-                inverse.append(1.0 / rows)
-            inverses.append((slot, m, inverse))
-        for slot, m, inverse in inverses:
-            for span in spans:
+                found.append(rows)
+            add_to(rows_acc, ms, slice(0, 128), found)
+            inverses.append([1.0 / rows for rows in found])
+        for span in spans:
+            totals = []
+            for j, slot in enumerate(slots):
                 tiles = [grad_buf[k, slot, :, span] for k in range(row_groups)]
-                add_to(weighted_acc, m, span, total_of([tile * tile * inverse[k] for k, tile in enumerate(tiles)]))
+                totals.append(total_of([tile * tile * inverses[k][j] for k, tile in enumerate(tiles)]))
+            add_to(weighted_acc, ms, span, totals)
         return carry
 
     lax.fori_loop(0, slot_count // group, work, 0)
@@ -196,18 +206,19 @@
         if c == 0:
             param_load(k).wait()
 
-        def slot(j, carry):
-            m = jnp.minimum(ids[j], mats - 1)
-            scale = scale_buf[k, j]
-            for s in range(parts):
-                span = slice(s * cut + c * 128, s * cut + (c + 1) * 128)
-                new = param_buf[k, j, :, span].astype(jnp.float32) - grad_buf[k, j, :, span] * scale * factor[m, :, span]
-                send_buf[u, s, j] = new.astype(send_buf.dtype)
-            return carry
-
-        lax.fori_loop(0, slot_count, slot, 0, unroll=unroll)
         spot = pl.ds(me * slot_count, slot_count)
         for core in (1, 0):
+
+            def slot(j, carry):
+                m = jnp.minimum(ids[j], mats - 1)
+                scale = scale_buf[k, j]
+                for s in range(core, parts, 2):
+                    span = slice(s * cut + c * 128, s * cut + (c + 1) * 128)
+                    new = param_buf[k, j, :, span].astype(jnp.float32) - grad_buf[k, j, :, span] * scale * factor[m, :, span]
+                    send_buf[u, s, j] = new.astype(send_buf.dtype)
+                return carry
+
+            lax.fori_loop(0, slot_count, slot, 0, unroll=unroll)
             for step in range(parts // 2):
                 to = lax.rem(me // 2 + step, parts // 2) * 2 + core
 
@@ -265,6 +276,9 @@
     early = min(units, 8)
     for u in range(early):
         update(u)
+        if u == 0:
+            for copy in small_stores:
+                copy.start()
     later = list(range(early, units))
     for i in range(units + copies - 2):
         if i < units:
@@ -306,6 +320,8 @@
         def _():
             wait(sent, line_send.at[1, h])
 
+    for copy in small_stores:
+        copy.wait()
     wait(temp_ref.at[0], own_sem)
     for u in range(units):
         wait(send_buf.at[u, pl.ds(0, parts - 1)], cross_send.at[u])
@@ -319,15 +335,23 @@
     return jnp.where(z >= copies - 2, 0, jnp.where(z <= 1, copies - 1, copies))
 
 
-def place_kernel(tail, cols_in, rows_in, in_ref, late_ref, cols_out, rows_out, out_ref, buf, group_load, group_store, load_sem, store_sem, late_load, late_store):
+def place_kernel(tail, cols_in, rows_in, in_ref, late_ref, cols_out, rows_out, out_ref, cols_buf, rows_buf, small_sem, buf, group_load, group_store, load_sem, store_sem, late_load, late_store):
     copies, row_groups = buf.shape[0], buf.shape[1]
     units = in_ref.shape[1]
     col_groups = units // row_groups
     skip = late_source(copies)
     z = lax.axis_index("dp")
     inner = (z == 1) | (z == copies - 2)
-    cols_out[...] = cols_in[...]
-    rows_out[...] = rows_in[...]
+    small_loads = [
+        pltpu.make_async_copy(cols_in, cols_buf, small_sem.at[0]),
+        pltpu.make_async_copy(rows_in, rows_buf, small_sem.at[1]),
+    ]
+    small_stores = [
+        pltpu.make_async_copy(cols_buf, cols_out, small_sem.at[2]),
+        pltpu.make_async_copy(rows_buf, rows_out, small_sem.at[3]),
+    ]
+    for copy in small_loads:
+        copy.start()
     full = (units - tail) // col_groups
     groups = [(k, d) for k in range(full) for d in range(copies)]
     singles = [(u, d) for u in range(full * col_groups, units) for d in range(copies)]
@@ -369,6 +393,9 @@
         for u in late_units:
             load_late(u).start()
 
+    for a, b in zip(small_loads, small_stores):
+        a.wait()
+        b.start()
     for k, d in groups:
         wait(buf.at[d, k], group_load.at[d, k])
         group_copy(k, d).start()
@@ -385,6 +412,8 @@
             load_late(u).wait()
             store_late(u).start()
 
+    for copy in small_stores:
+        copy.wait()
     for k, d in groups:
         group_copy(k, d).wait()
     for u, d in singles:
@@ -438,7 +467,7 @@
     new_cols, new_rows, temp, late = pl.pallas_call(
         functools.partial(main_kernel, mats, group, row_counts),
         in_specs=[smem, smem, smem, vmem, vmem, hbm, hbm],
-        out_specs=[vmem, vmem, hbm, hbm],
+        out_specs=[hbm, hbm, hbm, hbm],
         out_shape=[
             jax.ShapeDtypeStruct((mats, width), jnp.float32),
             jax.ShapeDtypeStruct((height, slot_count), jnp.float32),
@@ -469,6 +498,9 @@
             dma((2, copies - 1)),
             dma((2, copies - 1, units)),
             dma(()),
+            pltpu.VMEM((mats, width), jnp.float32),
+            pltpu.VMEM((height, slot_count), jnp.float32),
+            dma((4,)),
         ]
         + [pltpu.VMEM((parts * slot_count, CHUNK, 128), jnp.bfloat16) for _ in range(units)],
         compiler_params=pltpu.CompilerParams(
@@ -483,14 +515,17 @@
     placed_shape = jax.ShapeDtypeStruct((total_blocks, copies, chunks, CHUNK, cut), jnp.bfloat16)
     new_cols, new_rows, placed = pl.pallas_call(
         functools.partial(place_kernel, tail),
-        in_specs=[vmem, vmem, hbm, hbm],
-        out_specs=[vmem, vmem, hbm],
+        in_specs=[hbm, hbm, hbm, hbm],
+        out_specs=[hbm, hbm, hbm],
         out_shape=[
             jax.ShapeDtypeStruct((mats, width), jnp.float32),
             jax.ShapeDtypeStruct((height, slot_count), jnp.float32),
             placed_shape,
         ],
         scratch_shapes=[
+            pltpu.VMEM((mats, width), jnp.float32),
+            pltpu.VMEM((height, slot_count), jnp.float32),
+            dma((4,)),
             pltpu.VMEM((copies, chunks, total_blocks, CHUNK, cut), jnp.bfloat16),
             dma((copies, chunks)),
             dma((copies, chunks)),

time: 344 us -> 342 us (level)
  transfers between devices with their start and end apart: 1 -> 1, of which waited for: 0 -> 0; matrix products, arithmetic and copies ran while one was open for 0% -> 0% of each run, Pallas kernels for 5% -> 4%
where the time goes in v5:
time: 342 us; the launch traced here: 341 us
  Pallas kernels  339 us (99%)
    pallas_call x1, Pallas kernels, body(): pl.pallas_call(functools.partial(main_kernel, mats, group, row_counts), i...  324 us
    pallas_call x1, Pallas kernels, body(): pl.pallas_call(functools.partial(place_kernel, tail), in_specs=[hbm, hbm,...  13.9 us
  transfers between devices with their start and end apart: 1, of which 0 were waited for; matrix products, arithmetic and copies ran while one was open for 0% of the time, Pallas kernels for 4%

profile of v5, /device:TPU:0, one launch (start us, length us, event | category | flops | bytes accessed | tf_op | source)
XLA Modules:
  0.0 341.3 jit_solution(3027907540483133211)
XLA Ops:
  1.3 323.9 %main.1 = (f32[3,4096]{1,0:T(4,128)}, f32[32,36]{1,0:T(8,128)}, bf16[4,16,144,8,128]{4,3,2,1,0:T(8,128)(2,1)}, bf16[2,144,8,128]{3,2,1,0:T(8,128)(2,1)}) custom-call(s32[8]{0:T(128)} %start_ref.1, s32[144]{0:T(256)} %matrix_ref.1, s32[1]{0:T(128)S(6)} %copy.12.step_ref, f32[3,4096]{1,0:T(4,128)} %state_ref.1, f32[32,36]{1,0:T(8,128)} %bitcast.4, ...), custom_call_target="tpu_custom_call" | custom-call | flops 28311552 | bytes 37748736 | tf_op jit(solution)/shard_map/main/pallas_call | solution.py:467
  325.2 1.3 collective-permute-start
  326.5 13.9 %place.1 = (f32[3,4096]{1,0:T(4,128)}, f32[32,36]{1,0:T(8,128)}, bf16[144,4,4,8,512]{4,3,2,1,0:T(8,128)(2,1)}) custom-call(f32[3,4096]{1,0:T(4,128)} %get-tuple-element.11.cols_in, f32[32,36]{1,0:T(8,128)} %get-tuple-element.12.rows_in, bf16[4,16,144,8,128]{4,3,2,1,0:T(8,128)(2,1)} %get-tuple-element.13.in_ref, ...), custom_call_target="tpu_custom_call" | custom-call | flops 94371840 | bytes 37748736 | tf_op jit(solution)/shard_map/place/pallas_call | solution.py:516
  340.4 0.0 collective-permute-done.landed_ref
  340.4 0.8 place_late.1
Async XLA Ops:
  325.2 15.2 %collective-permute-start = (bf16[2,144,8,128]{3,2,1,0:T(8,128)(2,1)}, bf16[2,144,8,128]{3,2,1,0:T(8,128)(2,1)S(1)}, u32[]{:S(2)}, u32[]{:S(2)}) collective-permute-start(bf16[2,144,8,128]{3,2,1,0:T(8,128)(2,1)} %get-tuple-element.10.late_ref), channel_id=1, source_target_pairs={{2,3},{1,0},{6,7},{5,4},{10,11},{9,8},{14,15},{13,12},{18,19},{17,... | collective-permute-start | bytes 1769480 | tf_op jit(solution)/shard_map/ppermute | solution.py:513

commit v6 on v5

--- a/solution.py
+++ b/solution.py
@@ -273,7 +273,7 @@
         def _():
             pass_on(h, u, z + h, 1, z - 1, z == 2)
 
-    early = min(units, 8)
+    early = min(units, 4)
     for u in range(early):
         update(u)
         if u == 0:
@@ -456,7 +456,7 @@
     copies = lax.axis_size("dp")
     assert copies > 3
     units = chunks * (cut // 128)
-    tail = min(2, units - 1)
+    tail = min(3, units - 1)
     row_counts = (float(D), float(D), float(FF))
 
     smem = pl.BlockSpec(memory_space=pltpu.SMEM)

time: 342 us -> 341 us (level)
  Pallas kernels: 339 us -> 332 us
  waiting for transfers between devices: 0.01 us -> 5.54 us
    pallas_call x1, Pallas kernels: 324 us -> 318 us  [body(): pl.pallas_call(functools.partial(main_kernel, mats, group, row_counts), i...]
    ppermute x1, waiting for transfers between devices: 0.01 us -> 5.54 us  [body(): landed = lax.ppermute(late, 'dp', [(copies - 2, copies - 1), (1, 0)])]
  transfers between devices with their start and end apart: 1 -> 1, of which waited for: 0 -> 1; matrix products, arithmetic and copies ran while one was open for 0% -> 0% of each run, Pallas kernels for 4% -> 4%
where the time goes in v6:
time: 341 us; the launch traced here: 340 us
  Pallas kernels  332 us (97%)
  waiting for transfers between devices  5.54 us (2%)
    pallas_call x1, Pallas kernels, body(): pl.pallas_call(functools.partial(main_kernel, mats, group, row_counts), i...  318 us
    pallas_call x1, Pallas kernels, body(): pl.pallas_call(functools.partial(place_kernel, tail), in_specs=[hbm, hbm,...  13.8 us
  transfers between devices with their start and end apart: 1, of which 1 were waited for; matrix products, arithmetic and copies ran while one was open for 0% of the time, Pallas kernels for 4%

profile of v6, /device:TPU:0, one launch (start us, length us, event | category | flops | bytes accessed | tf_op | source)
XLA Modules:
  0.0 340.4 jit_solution(15221229199780716025)
XLA Ops:
  1.3 317.6 %main.1 = (f32[3,4096]{1,0:T(4,128)}, f32[32,36]{1,0:T(8,128)}, bf16[4,16,144,8,128]{4,3,2,1,0:T(8,128)(2,1)}, bf16[3,144,8,128]{3,2,1,0:T(8,128)(2,1)}) custom-call(s32[8]{0:T(128)} %start_ref.1, s32[144]{0:T(256)} %matrix_ref.1, s32[1]{0:T(128)S(6)} %copy.12.step_ref, f32[3,4096]{1,0:T(4,128)} %state_ref.1, f32[32,36]{1,0:T(8,128)} %bitcast.4, ...), custom_call_target="tpu_custom_call" | custom-call | flops 28311552 | bytes 37748736 | tf_op jit(solution)/shard_map/main/pallas_call | solution.py:467
  318.9 1.3 collective-permute-start
  320.2 13.8 %place.1 = (f32[3,4096]{1,0:T(4,128)}, f32[32,36]{1,0:T(8,128)}, bf16[144,4,4,8,512]{4,3,2,1,0:T(8,128)(2,1)}) custom-call(f32[3,4096]{1,0:T(4,128)} %get-tuple-element.11.cols_in, f32[32,36]{1,0:T(8,128)} %get-tuple-element.12.rows_in, bf16[4,16,144,8,128]{4,3,2,1,0:T(8,128)(2,1)} %get-tuple-element.13.in_ref, ...), custom_call_target="tpu_custom_call" | custom-call | flops 94371840 | bytes 37748736 | tf_op jit(solution)/shard_map/place/pallas_call | solution.py:516
  334.0 5.5 %collective-permute-done.landed_ref = bf16[3,144,8,128]{3,2,1,0:T(8,128)(2,1)S(1)} collective-permute-done((bf16[3,144,8,128]{3,2,1,0:T(8,128)(2,1)}, bf16[3,144,8,128]{3,2,1,0:T(8,128)(2,1)S(1)}, u32[]{:S(2)}, u32[]{:S(2)}) %collective-permute-start) | collective-permute-done | bytes 884768 | tf_op jit(solution)/shard_map/ppermute | solution.py:513
  339.5 0.9 place_late.1
Async XLA Ops:
  318.9 20.6 %collective-permute-start = (bf16[3,144,8,128]{3,2,1,0:T(8,128)(2,1)}, bf16[3,144,8,128]{3,2,1,0:T(8,128)(2,1)S(1)}, u32[]{:S(2)}, u32[]{:S(2)}) collective-permute-start(bf16[3,144,8,128]{3,2,1,0:T(8,128)(2,1)} %get-tuple-element.10.late_ref), channel_id=1, source_target_pairs={{2,3},{1,0},{6,7},{5,4},{10,11},{9,8},{14,15},{13,12},{18,19},{17,... | collective-permute-start | bytes 2654216 | tf_op jit(solution)/shard_map/ppermute | solution.py:513
